TPU v7x, 32 devices: a whole 2x2x4 slice. The times are simulated.
32 devices in a mesh: gx: 4 (over y, x), gy: 8 (over z, core).
Axes of the slice: x: 2, y: 2, z: 4, core: 2. Of those that a mesh axis runs over, the one named last changes fastest.
Arguments:
- right_side: float32 [256, 256, 256], P('gx', 'gy'), may hold values from -45 to 45
- block_inverse: float32 [1, 256, 256], replicated, may hold values from -1 to 2
- basis_left: float32 [2, 1, 32, 256], replicated, may hold values from -0.25 to 0.25
- basis_right: float32 [2, 1, 32, 256], replicated, may hold values from -0.25 to 0.25
- ranks: int32 [2, 1, 256, 256], replicated, may hold values from 1 to 32
Outputs:
- solution_field: float32 [256, 256, 256], P('gx', 'gy')
- true_gap: float32 [256, 256, 256], P('gx', 'gy')
- preconditioned: float32 [256, 256, 256], P('gx', 'gy')
All inputs are finite; a program needn't handle non-finite values.
Results may differ from a plain program's by a relative error of at most 0.0003.
Values sent between devices are 32-bit elements; how exact they have to be, the bound alone decides.
No kernel may reach another device: no remote copies, remote signals or barrier semaphores. Data moves between devices by JAX's collectives and lax.ppermute only.
A program may use at most 64 MiB of HBM per device.

v0:
```python
import jax
import jax.numpy as jnp
from jax import lax
from jax.experimental import pallas as pl
from jax.experimental.pallas import tpu as pltpu
from jax.sharding import PartitionSpec as P

F32 = jnp.float32
BF16 = jnp.bfloat16
DIAGONAL = 6.0 + 0.05
DEPTH = 5
PAD = 8
NT = (((1,), (1,)), ((), ()))
NN = (((1,), (0,)), ((), ()))
TN = (((0,), (0,)), ((), ()))
WHOLE = pl.BlockSpec(memory_space=pltpu.VMEM)
GRANT = pltpu.CompilerParams(vmem_limit_bytes=16 << 20)


def largest_divisor(count, limit):
    return max(d for d in range(1, limit + 1) if count % d == 0)


def dot(left, right, dims):
    return lax.dot_general(left, right, dims, preferred_element_type=F32)


def halves(value):
    high = value.astype(BF16)
    low = (value - high.astype(F32)).astype(BF16)
    return high, low


def inward(inverse, left, right):
    square = halves(inverse[0])
    factors = jnp.concatenate([right[0, 0], left[0, 0], right[1, 0], left[1, 0]], 0)
    narrow = halves(factors)
    return square, (jnp.concatenate(narrow, 0), narrow[0])


def outward(left, right):
    factors = jnp.concatenate([left[0, 0], right[0, 0], left[1, 0], right[1, 0]], 0)
    high, low = halves(factors)
    return jnp.concatenate([high, high], 0), low


def diagonal_part(high, low, square):
    return dot(high, square[0], NT) + dot(high, square[1], NT) + dot(low, square[0], NT)


def coefficients(high, low, narrow):
    both = dot(high, narrow[0], NT)
    rank = both.shape[1] // 2
    return both[:, :rank] + both[:, rank:] + dot(low, narrow[1], NT)


def coupling_part(coefs, factors):
    high, low = halves(coefs)
    return dot(jnp.concatenate([high, low], 1), factors[0], NN) + dot(high, factors[1], NN)


def gathered(coef_ref, start, rows, stride, limit):
    here = coef_ref[pl.ds(start, rows)]
    lane = lax.broadcasted_iota(jnp.int32, here.shape, 1)
    quarter = here.shape[1] // 4
    ahead_x = coef_ref[pl.ds(pl.multiple_of(start + stride, 8), rows)]
    behind_x = coef_ref[pl.ds(pl.multiple_of(start - stride, 8), rows)]
    ahead_y = pltpu.roll(here, rows - 1, 0)
    behind_y = pltpu.roll(here, 1, 0)
    along_x = jnp.where(lane < quarter, ahead_x, behind_x)
    along_y = jnp.where(lane < 3 * quarter, ahead_y, behind_y)
    picked = jnp.where(lane < 2 * quarter, along_x, along_y)
    level = lax.rem(lane, quarter).astype(F32)
    return jnp.where(level < limit, picked, 0.0)


def operated(ref, start, rows, stride):
    here = ref[pl.ds(start, rows)]
    width = here.shape[1]
    beside = ref[pl.ds(pl.multiple_of(start + stride, 8), rows)]
    beside = beside + ref[pl.ds(pl.multiple_of(start - stride, 8), rows)]
    beside = beside + pltpu.roll(here, rows - 1, 0) + pltpu.roll(here, 1, 0)
    beside = beside + pltpu.roll(here, width - 1, 1) + pltpu.roll(here, 1, 1)
    return DIAGONAL * here - beside


def own_kernel(stride, block, inverse, left, right, diag_out, coef_out):
    cells_x, cells_y, width = block.shape
    square, narrow = inward(inverse, left, right)
    step = largest_divisor(cells_x, 8)

    def body(i, carry):
        rows = block[pl.ds(i * step, step)].reshape(step * cells_y, width)
        high, low = halves(rows)
        diag = diagonal_part(high, low, square)
        coef = coefficients(high, low, narrow)
        for j in range(step):
            at = pl.multiple_of((i * step + j + DEPTH) * stride + PAD, 8)
            diag_out[pl.ds(at, cells_y)] = diag[j * cells_y : (j + 1) * cells_y]
            coef_out[pl.ds(at, cells_y)] = coef[j * cells_y : (j + 1) * cells_y]
        return carry

    lax.fori_loop(0, cells_x // step, body, 0)


def side_kernel(stride, diag_in, coef_in, low_x, high_x, low_y, high_y, inverse, left, right, diag_out, coef_out, turned):
    square, narrow = inward(inverse, left, right)
    depth, cells_y, width = low_x.shape
    cells_x = low_y.shape[1]
    for ref, first in ((low_x, 0), (high_x, DEPTH + cells_x)):
        high, low = halves(ref[...].reshape(depth * cells_y, width))
        diag = diagonal_part(high, low, square)
        coef = coefficients(high, low, narrow)
        for j in range(depth):
            at = (first + j) * stride + PAD
            diag_out[pl.ds(at, cells_y)] = diag[j * cells_y : (j + 1) * cells_y]
            coef_out[pl.ds(at, cells_y)] = coef[j * cells_y : (j + 1) * cells_y]
    for ref, inside, edge in ((low_y, PAD - DEPTH, 0), (high_y, 0, PAD + cells_y)):
        high, low = halves(ref[...].reshape(depth * cells_x, width))
        diag = diagonal_part(high, low, square)
        coef = coefficients(high, low, narrow)
        for j in range(depth):
            part = slice(j * cells_x, (j + 1) * cells_x)
            at = pl.ds(inside + j, cells_x, stride=PAD)
            for k in range(width // 128):
                turned[k, at] = diag[part, k * 128 : (k + 1) * 128]
            turned[width // 128, at] = coef[part]

        def place(x, carry):
            here = pl.ds(pl.multiple_of(x * PAD, 8), PAD)
            at = pl.ds(pl.multiple_of((x + DEPTH) * stride + edge, 8), PAD)
            for k in range(width // 128):
                diag_out[at, pl.ds(k * 128, 128)] = turned[k, here]
            coef_out[at] = turned[width // 128, here]
            return carry

        lax.fori_loop(0, cells_x, place, 0, unroll=4)


def chain_kernel(
    stride, diag_in, coef_in, low_x, high_x, limits, block, inverse, left, right,
    first, coef, first_image, second, second_image, limit, sums,
):
    cells_x, cells_y, width = block.shape
    square, narrow = inward(inverse, left, right)
    factors = outward(left, right)
    near = DEPTH - 1

    for ref, edge, sign in ((low_x, DEPTH - near, -1), (high_x, DEPTH + cells_x, 1)):
        count = ref.shape[0] * ref.shape[1]
        high, low = halves(ref[...].reshape(count, width))
        diag = diagonal_part(high, low, square)
        coefs = coefficients(high, low, narrow)
        for j in range(2 * near):
            away_y = near - j if j < near else j - near + 1
            y = PAD - away_y if j < near else PAD + cells_y + away_y - 1
            for i in range(near):
                away_x = near - i if sign < 0 else i + 1
                if away_x + away_y <= DEPTH:
                    at = (edge + i) * stride + y
                    row = j * near + i
                    first[pl.ds(at, 1)] = diag[row : row + 1]
                    coef[pl.ds(at, 1)] = coefs[row : row + 1]

    kinds = limits.shape[0]
    lane = lax.broadcasted_iota(jnp.int32, (kinds, coef.shape[1]), 1)
    kind = lax.broadcasted_iota(jnp.int32, (kinds, coef.shape[1]), 0)
    spread = jnp.where(lane // (coef.shape[1] // 4) == kind, 1.0, 0.0).astype(BF16)

    def spread_limits(i, carry):
        at = pl.multiple_of(i * 128, 128)
        limit[pl.ds(at, 128)] = dot(limits[:, pl.ds(at, 128)], spread, TN)
        return carry

    lax.fori_loop(0, limits.shape[1] // 128, spread_limits, 0)

    def slabs(begin, end, most, work):
        step = largest_divisor(end - begin, most)

        def body(i, carry):
            return work(pl.multiple_of((begin + i * step) * stride, 8), step * stride, carry)

        return body, (end - begin) // step

    def couple(ref):
        def work(start, rows, carry):
            at = pl.ds(start, rows)
            picked = gathered(coef, start, rows, stride, limit[at])
            ref[at] = ref[at] + coupling_part(picked, factors)
            return carry

        return work

    def image_and_project(start, rows, carry):
        at = pl.ds(start, rows)
        image = operated(first, start, rows, stride)
        first_image[at] = image
        high, low = halves(image)
        second[at] = diagonal_part(high, low, square)
        coef[at] = coefficients(high, low, narrow)
        return carry

    def last_image(start, rows, carry):
        second_image[pl.ds(start, rows)] = operated(second, start, rows, stride)
        return carry

    last = 2 * DEPTH + cells_x
    body, count = slabs(1, last - 1, 9, couple(first))
    lax.fori_loop(0, count, body, 0)
    body, count = slabs(2, last - 2, 9, image_and_project)
    lax.fori_loop(0, count, body, 0)
    body, count = slabs(3, last - 3, 9, couple(second))
    lax.fori_loop(0, count, body, 0)
    body, count = slabs(4, last - 4, 9, last_image)
    lax.fori_loop(0, count, body, 0)

    def fold(value):
        return jnp.sum(value.reshape(cells_y // 8, 8, width), 0)

    def products(x, carry):
        at = pl.ds(pl.multiple_of((x + DEPTH) * stride + PAD, 8), cells_y)
        rhs = block[x]
        z0, w0, u0, v0 = first[at], first_image[at], second[at], second_image[at]
        terms = (rhs * z0, z0 * w0, rhs * u0, w0 * u0, u0 * v0)
        return tuple(c + fold(t) for c, t in zip(carry, terms))

    zero = jnp.zeros((8, width), F32)
    parts = lax.fori_loop(0, cells_x, products, (zero,) * 5)
    rows = [jnp.sum(jnp.sum(p, 0, keepdims=True), 1, keepdims=True) for p in parts]
    for i, row in enumerate(rows):
        sums[pl.ds(i, 1)] = jnp.broadcast_to(row, (1, sums.shape[1]))
    sums[pl.ds(5, 3)] = jnp.zeros((3, sums.shape[1]), F32)


def last_kernel(stride, begin, field, limit, inverse, left, right, out, coef):
    step, cells_y, width = out.shape
    square, narrow = inward(inverse, left, right)
    factors = outward(left, right)
    start = (begin + DEPTH) * stride
    high, low = halves(field[pl.ds(start - stride, (step + 2) * stride)])
    coef[...] = coefficients(high, low, narrow)
    picked = gathered(coef, stride, step * stride, stride, limit[pl.ds(start, step * stride)])
    picked = picked.reshape(step, stride, picked.shape[1])[:, PAD : PAD + cells_y]
    rows = field[pl.ds(start, step * stride)].reshape(step, stride, width)[:, PAD : PAD + cells_y]
    high, low = halves(rows.reshape(step * cells_y, width))
    total = diagonal_part(high, low, square)
    total = total + coupling_part(picked.reshape(step * cells_y, picked.shape[2]), factors)
    out[...] = total.reshape(step, cells_y, width)


def combine_kernel(stride, step, pieces, sums, block, z_ref, w_ref, u_ref, v_ref, *rest):
    y_refs, (solution_out, gap_out, precond_out) = rest[:pieces], rest[pieces:]
    i = pl.program_id(0)
    cells_y = block.shape[1]
    rz, zw, ru, wu, uv = (sums[pl.ds(k, 1), pl.ds(0, 128)] for k in range(5))
    alpha = rz / zw
    rz_next = alpha * (alpha * wu - ru)
    ratio = rz_next / rz
    grown = 1.0 + ratio
    curve = grown * (grown * zw - 2.0 * alpha * wu) + alpha * alpha * uv
    alpha_next = rz_next / curve
    s = jnp.concatenate([alpha + alpha_next * grown] * (block.shape[2] // 128), 1)
    t = jnp.concatenate([alpha * alpha_next] * (block.shape[2] // 128), 1)

    def work(y_ref):
        for j in range(step):
            x = i * step + j
            at = pl.ds(pl.multiple_of((x + DEPTH) * stride + PAD, 8), cells_y)
            z0, w0, u0, v0 = z_ref[at], w_ref[at], u_ref[at], v_ref[at]
            solution_out[j] = s * z0 - t * u0
            gap_out[j] = (block[j] - s * w0) + t * v0
            precond_out[j] = (z0 - s * u0) + t * y_ref[lax.rem(x, y_ref.shape[0])]

    per = y_refs[0].shape[0] // step
    for k in range(pieces):
        pl.when(lax.div(i, per) == k)(lambda k=k: work(y_refs[k]))


def resident(*values):
    return tuple(pltpu.with_memory_space_constraint(v, pltpu.VMEM) for v in values)


def neighbour(value, axis, offset):
    count = lax.axis_size(axis)
    return lax.ppermute(value, axis, [(i, (i + offset) % count) for i in range(count)])


def wrapped(table, axis, begin, size, before, after):
    length = table.shape[axis]
    head = lax.slice_in_dim(table, length - before, length, axis=axis)
    tail = lax.slice_in_dim(table, 0, after, axis=axis)
    whole = jnp.concatenate([head, table, tail], axis)
    return lax.dynamic_slice_in_dim(whole, begin, size + before + after, axis)


def total_over(value, axis):
    count = lax.axis_size(axis)
    if count & (count - 1):
        return lax.psum(value, axis)
    hop = 1
    while hop < count:
        value = value + lax.ppermute(value, axis, [(i, i ^ hop) for i in range(count)])
        hop *= 2
    return value


def per_device(right_side, block_inverse, basis_left, basis_right, ranks):
    cells_x, cells_y, width = right_side.shape
    stride = cells_y + 2 * PAD
    lines = (cells_x + 2 * DEPTH) * stride
    padded = -(-lines // 128) * 128
    rank4 = 4 * basis_left.shape[2]
    weights = (block_inverse, basis_left, basis_right)
    wide = pltpu.VMEM((lines, width), F32)
    slim = pltpu.VMEM((lines, rank4), F32)

    low_y = neighbour(jnp.transpose(right_side[:, cells_y - DEPTH :], (1, 0, 2)), "gy", 1)
    high_y = neighbour(jnp.transpose(right_side[:, :DEPTH], (1, 0, 2)), "gy", -1)
    low_x = neighbour(right_side[cells_x - DEPTH :], "gx", 1)
    high_x = neighbour(right_side[:DEPTH], "gx", -1)

    diag, coef = pl.pallas_call(
        lambda *refs: own_kernel(stride, *refs),
        out_shape=(wide, slim), in_specs=[WHOLE] * 4, out_specs=(WHOLE,) * 2, name="own", compiler_params=GRANT,
    )(*resident(right_side, *weights))

    table = wrapped(ranks[:, 0], 1, lax.axis_index("gx") * cells_x, cells_x, DEPTH + 1, DEPTH)
    table = wrapped(table, 2, lax.axis_index("gy") * cells_y, cells_y, PAD + 1, PAD)
    limits = jnp.stack([table[0, 1:, 1:], table[0, :-1, 1:], table[1, 1:, 1:], table[1, 1:, :-1]])
    limits = jnp.pad(limits.reshape(4, lines).astype(F32), ((0, 4), (0, padded - lines))).astype(BF16)

    near = DEPTH - 1
    corners = jnp.concatenate([low_y[1:], high_y[:near]], 0)
    corner_low = neighbour(corners[:, cells_x - near :], "gx", 1)
    corner_high = neighbour(corners[:, :near], "gx", -1)

    diag, coef = pl.pallas_call(
        lambda *refs: side_kernel(stride, *refs),
        out_shape=(wide, slim), in_specs=[WHOLE] * 9, out_specs=(WHOLE,) * 2,
        input_output_aliases={0: 0, 1: 1}, name="side", compiler_params=GRANT,
        scratch_shapes=[pltpu.VMEM((width // 128 + 1, cells_x * PAD, 128), F32)],
    )(*resident(diag, coef, low_x, high_x, low_y, high_y, *weights))

    first, _, first_image, second, second_image, limit, sums = pl.pallas_call(
        lambda *refs: chain_kernel(stride, *refs),
        out_shape=(
            wide, slim, wide, wide, wide,
            pltpu.VMEM((padded, rank4), F32), pltpu.VMEM((8, 128), F32),
        ),
        in_specs=[WHOLE] * 9, out_specs=(WHOLE,) * 7,
        input_output_aliases={0: 0, 1: 1}, name="chain", compiler_params=GRANT,
    )(*resident(diag, coef, corner_low, corner_high, limits, right_side, *weights))

    sums = total_over(total_over(sums, "gx"), "gy")

    pieces = 4 if cells_x % 4 == 0 else 1
    step = cells_x // pieces
    last = [
        pl.pallas_call(
            lambda *refs, k=k: last_kernel(stride, k * step, *refs),
            out_shape=pltpu.VMEM((step, cells_y, width), F32),
            in_specs=[WHOLE] * 5, out_specs=WHOLE,
            scratch_shapes=[pltpu.VMEM(((step + 2) * stride, rank4), F32)], name="last", compiler_params=GRANT,
        )(*resident(second_image, limit, *weights))
        for k in range(pieces)
    ]

    chunk = largest_divisor(step, 8)
    tile = pl.BlockSpec((chunk, cells_y, width), lambda i: (i, 0, 0))
    out = jax.ShapeDtypeStruct((cells_x, cells_y, width), F32)
    return pl.pallas_call(
        lambda *refs: combine_kernel(stride, chunk, pieces, *refs),
        grid=(cells_x // chunk,),
        out_shape=(out,) * 3,
        in_specs=[WHOLE, tile] + [WHOLE] * (4 + pieces), out_specs=(tile,) * 3, name="combine", compiler_params=GRANT,
    )(*resident(sums), right_side, *resident(first, first_image, second, second_image, *last))


def solution(mesh):
    placed = (P("gx", "gy", None), P(), P(), P(), P())
    return jax.shard_map(
        per_device,
        mesh=mesh,
        in_specs=placed,
        out_specs=(P("gx", "gy", None), P("gx", "gy", None), P("gx", "gy", None)),
        check_vma=False,
    )
```

profile of v0, /device:TPU:0, one launch (start us, length us, event | category | flops | bytes accessed | tf_op | source)
XLA Modules:
  0.0 74.1 jit_solution(10350790047501038622)
XLA Ops:
  0.6 1.7 %fusion.6 = (f32[5,32,256]{2,1,0:T(8,128)}, f32[5,32,256]{2,1,0:T(8,128)}) fusion(f32[64,32,256]{2,1,0:T(8,128)} %refs_1_.3), kind=kLoop, calls=%fused_computation.17 | loop fusion | bytes 655360 | tf_op jit(solution)/shard_map/slice | solution.py:320
  2.4 3.9 %collective-permute-start.1 = (f32[5,32,256]{2,1,0:T(8,128)}, f32[5,32,256]{2,1,0:T(8,128)S(1)}, u32[]{:S(2)}, u32[]{:S(2)}) collective-permute-start(f32[5,32,256]{2,1,0:T(8,128)} %get-tuple-element.25), channel_id=1, source_target_pairs={{0,24},{8,0},{16,8},{24,16},{1,25},{9,1},{17,9},{25,17},{2,26},{10... | collective-permute-start | bytes 491528 | tf_op jit(solution)/shard_map/ppermute | solution.py:285
  6.3 0.0 collective-permute-start
  6.3 1.3 %fusion.5 = (f32[64,5,256]{2,1,0:T(8,128)S(1)}, f32[64,5,256]{2,1,0:T(8,128)S(1)}) fusion(f32[64,32,256]{2,1,0:T(8,128)} %refs_1_.3), kind=kLoop, calls=%fused_computation.16 | loop fusion | bytes 1310720 | tf_op jit(solution)/shard_map/slice | solution.py:318
  7.6 0.8 %copy.21 = f32[64,5,256]{2,0,1:T(8,128)} copy(f32[64,5,256]{2,1,0:T(8,128)S(1)} %get-tuple-element.24) | data formatting | bytes 655360
  8.4 0.0 collective-permute-start.2
  8.4 0.8 %copy.20 = f32[64,5,256]{2,0,1:T(8,128)} copy(f32[64,5,256]{2,1,0:T(8,128)S(1)} %get-tuple-element.23) | data formatting | bytes 655360
  9.2 0.0 copy-start
  9.2 0.0 copy-start.1
  9.2 0.0 copy-start.2
  9.2 0.0 copy-start.3
  9.2 3.6 %collective-permute-start.3 = (f32[5,64,256]{2,1,0:T(8,128)}, f32[5,64,256]{2,1,0:T(8,128)S(1)}, u32[]{:S(2)}, u32[]{:S(2)}) collective-permute-start(f32[5,64,256]{2,1,0:T(8,128)} %bitcast.5), channel_id=1, source_target_pairs={{0,7},{1,0},{2,1},{3,2},{4,3},{5,4},{6,5},{7,6},{8,15},{9,8},{10,9... | collective-permute-start | bytes 983048 | tf_op jit(solution)/shard_map/ppermute | solution.py:285
  12.8 0.7 slice.67
  13.5 0.7 slice.66
  14.3 1.0 %fusion.1 = s32[2,75,256]{2,1,0:T(8,128)S(1)} fusion(s32[]{:T(128)S(6)} %select_n.6, s32[2,6,256]{2,1,0:T(8,128)S(1)} %slice.66, s32[2,256,256]{2,1,0:T(8,128)} %bitcast.9, s32[2,5,256]{2,1,0:T(8,128)S(1)} %slice.67), kind=kLoop, calls=%fused_computation.9 | loop fusion | flops 76800 | bytes 700420 | tf_op jit(solution)/shard_map/concatenate | solution.py:292
  15.2 0.0 copy-start.4
  15.3 0.6 copy-done.4
  15.9 0.7 slice.68
  16.6 1.1 %fusion.4 = s32[2,75,49]{2,1,0:T(8,128)S(1)} fusion(s32[]{:T(128)S(6)} %select_n.7, s32[2,75,9]{2,1,0:T(8,128)} %slice.68, s32[2,75,256]{2,1,0:T(8,128)} %copy-done.4, s32[2,75,8]{2,1,0:T(8,128)S(1)} %slice.69), kind=kLoop, calls=%fused_computation.13 | loop fusion | flops 14700 | bytes 193204 | tf_op jit(solution)/shard_map/concatenate | solution.py:292
  17.7 0.1 fusion.7
  17.8 0.0 collective-permute-done.2.refs_4_
  17.9 0.0 collective-permute-done.3.refs_5_
  17.9 0.6 pad_maximum_fusion
  18.5 2.9 %collective-permute-start.5 = (f32[8,4,256]{2,1,0:T(4,128)}, f32[8,4,256]{2,1,0:T(4,128)S(1)}, u32[]{:S(2)}, u32[]{:S(2)}) collective-permute-start(f32[8,4,256]{2,1,0:T(4,128)} %get-tuple-element.27), channel_id=1, source_target_pairs={{0,24},{8,0},{16,8},{24,16},{1,25},{9,1},{17,9},{25,17},{2,26},{10... | collective-permute-start | bytes 98312 | tf_op jit(solution)/shard_map/ppermute | solution.py:285
  21.4 0.0 collective-permute-start.4
  21.4 0.7 fusion.2
  22.1 1.6 %convert_element_type.10 = bf16[4,3552]{1,0:T(4,128)(2,1)} reshape(bf16[4,74,48]{2,1,0:T(8,128)(2,1)} %fusion.2) | data formatting | bytes 56832 | tf_op jit(solution)/shard_map/convert_element_type | solution.py:330
  23.7 0.8 %pad.5.refs_4_ = bf16[8,3584]{1,0:T(8,128)(2,1)S(1)} pad(bf16[4,3552]{1,0:T(4,128)(2,1)} %convert_element_type.10, bf16[]{:T(256)} %constant.20.clone.1), padding=0_4x0_32 | pad | bytes 85762 | tf_op jit(solution)/shard_map/jit(_pad)/pad | solution.py:330
  24.5 0.0 copy-done
  24.5 0.0 copy-done.1
  24.5 0.0 copy-done.2
  24.5 0.0 copy-done.3
  24.5 3.3 %own.1 = (f32[3552,256]{1,0:T(8,128)S(1)}, f32[3552,128]{1,0:T(8,128)S(1)}) custom-call(f32[64,32,256]{2,1,0:T(8,128)S(1)} %copy-done, f32[1,256,256]{2,1,0:T(8,128)S(1)} %copy-done.1, f32[2,1,32,256]{3,2,1,0:T(8,128)S(1)} %copy-done.2, f32[2,1,32,256]{3,2,1,0:T(8,128)S(1)} %copy-done.3), custom_call_target="tpu_custom_call" | custom-call | tf_op jit(solution)/shard_map/own/pallas_call | solution.py:322
  27.8 0.0 collective-permute-done.1.refs_3_
  27.8 0.0 collective-permute-done.refs_2_
  27.9 1.6 %side.1 = (f32[3552,256]{1,0:T(8,128)S(1)}, f32[3552,128]{1,0:T(8,128)S(1)}) custom-call(f32[3552,256]{1,0:T(8,128)S(1)} %get-tuple-element.13.refs_0_, f32[3552,128]{1,0:T(8,128)S(1)} %get-tuple-element.14.refs_1_, f32[5,32,256]{2,1,0:T(8,128)S(1)} %collective-permute-done.refs_2_, ...), custom_call_target="tpu_custom_call", output_to_operand_aliasing={{0}: (0, {}), {1}: (1, {})} | custom-call | tf_op jit(solution)/shard_map/side/pallas_call | solution.py:337
  29.5 0.0 collective-permute-done.5.refs_3_
  29.5 0.0 collective-permute-done.4.refs_2_
  29.5 21.1 %chain.1 = (f32[3552,256]{1,0:T(8,128)S(1)}, f32[3552,128]{1,0:T(8,128)S(1)}, f32[3552,256]{1,0:T(8,128)S(1)}, f32[3552,256]{1,0:T(8,128)S(1)}, f32[3552,256]{1,...) custom-call(f32[3552,256]{1,0:T(8,128)S(1)} %get-tuple-element.15.ref, ...), custom_call_target="tpu_custom_call", output_to_operand_aliasing={{0}: (0, {}), {1}: (1, {})} | custom-call | tf_op jit(solution)/shard_map/chain/pallas_call | solution.py:344
  50.6 2.0 %collective-permute-start.6 = (f32[8,128]{1,0:T(8,128)S(1)}, f32[8,128]{1,0:T(8,128)S(1)}, u32[]{:S(2)}, u32[]{:S(2)}) collective-permute-start(f32[8,128]{1,0:T(8,128)S(1)} %get-tuple-element.17), channel_id=1, source_target_pairs={{0,8},{8,0},{16,24},{24,16},{1,9},{9,1},{17,25},{25,17},{2,10},{10... | collective-permute-start | bytes 12296 | tf_op jit(solution)/shard_map/ppermute | solution.py:302
  52.6 1.6 %collective-permute-done.6 = f32[8,128]{1,0:T(8,128)S(1)} collective-permute-done((f32[8,128]{1,0:T(8,128)S(1)}, f32[8,128]{1,0:T(8,128)S(1)}, u32[]{:S(2)}, u32[]{:S(2)}) %collective-permute-start.6) | collective-permute-done | bytes 4128 | tf_op jit(solution)/shard_map/ppermute | solution.py:302
  54.3 1.5 %collective-permute-start.7 = (f32[8,128]{1,0:T(8,128)S(1)}, f32[8,128]{1,0:T(8,128)S(1)}, u32[]{:S(2)}, u32[]{:S(2)}) collective-permute-start(f32[8,128]{1,0:T(8,128)S(1)} %add.25), channel_id=1, source_target_pairs={{0,16},{8,24},{16,0},{24,8},{1,17},{9,25},{17,1},{25,9},{2,18},{10... | collective-permute-start | bytes 12296 | tf_op jit(solution)/shard_map/ppermute | solution.py:302
  55.7 2.2 %collective-permute-done.7 = f32[8,128]{1,0:T(8,128)S(1)} collective-permute-done((f32[8,128]{1,0:T(8,128)S(1)}, f32[8,128]{1,0:T(8,128)S(1)}, u32[]{:S(2)}, u32[]{:S(2)}) %collective-permute-start.7) | collective-permute-done | bytes 4128 | tf_op jit(solution)/shard_map/ppermute | solution.py:302
  57.9 0.1 collective-permute-start.8
  58.0 1.1 %collective-permute-done.8 = f32[8,128]{1,0:T(8,128)S(1)} collective-permute-done((f32[8,128]{1,0:T(8,128)S(1)}, f32[8,128]{1,0:T(8,128)S(1)}, u32[]{:S(2)}, u32[]{:S(2)}) %collective-permute-start.8) | collective-permute-done | bytes 4128 | tf_op jit(solution)/shard_map/ppermute | solution.py:302
  59.1 2.2 %collective-permute-start.9 = (f32[8,128]{1,0:T(8,128)S(1)}, f32[8,128]{1,0:T(8,128)S(1)}, u32[]{:S(2)}, u32[]{:S(2)}) collective-permute-start(f32[8,128]{1,0:T(8,128)S(1)} %add.27), channel_id=1, source_target_pairs={{0,2},{1,3},{2,0},{3,1},{4,6},{5,7},{6,4},{7,5},{8,10},{9,11},{10,... | collective-permute-start | bytes 12296 | tf_op jit(solution)/shard_map/ppermute | solution.py:302
  61.2 1.6 %collective-permute-done.9 = f32[8,128]{1,0:T(8,128)S(1)} collective-permute-done((f32[8,128]{1,0:T(8,128)S(1)}, f32[8,128]{1,0:T(8,128)S(1)}, u32[]{:S(2)}, u32[]{:S(2)}) %collective-permute-start.9) | collective-permute-done | bytes 4128 | tf_op jit(solution)/shard_map/ppermute | solution.py:302
  62.8 3.2 %collective-permute-start.10 = (f32[8,128]{1,0:T(8,128)S(1)}, f32[8,128]{1,0:T(8,128)S(1)}, u32[]{:S(2)}, u32[]{:S(2)}) collective-permute-start(f32[8,128]{1,0:T(8,128)S(1)} %add.28), channel_id=1, source_target_pairs={{0,4},{1,5},{2,6},{3,7},{4,0},{5,1},{6,2},{7,3},{8,12},{9,13},{10,... | collective-permute-start | bytes 12296 | tf_op jit(solution)/shard_map/ppermute | solution.py:302
  66.0 0.9 %last.7.refs_9_ = f32[16,32,256]{2,1,0:T(8,128)S(1)} custom-call(f32[3552,256]{1,0:T(8,128)S(1)} %get-tuple-element.21.refs_0_.refs_5_, f32[3584,128]{1,0:T(8,128)S(1)} %get-tuple-element.22.refs_1_, f32[1,256,256]{2,1,0:T(8,128)S(1)} %copy-done.1, f32[2,1,32,256]{3,2,1,0:T(8,128)S(1)} %copy-done.2, f32[2,1,32,256]{3,2,1,0:T(8,128)S(1)} %copy-done.3), custom_call_target="tpu_custom_call" | custom-call | tf_op jit(solution)/shard_map/last/pallas_call | solution.py:359
  67.0 0.9 %last.6.refs_8_ = f32[16,32,256]{2,1,0:T(8,128)S(1)} custom-call(f32[3552,256]{1,0:T(8,128)S(1)} %get-tuple-element.21.refs_0_.refs_5_, f32[3584,128]{1,0:T(8,128)S(1)} %get-tuple-element.22.refs_1_, f32[1,256,256]{2,1,0:T(8,128)S(1)} %copy-done.1, f32[2,1,32,256]{3,2,1,0:T(8,128)S(1)} %copy-done.2, f32[2,1,32,256]{3,2,1,0:T(8,128)S(1)} %copy-done.3), custom_call_target="tpu_custom_call" | custom-call | tf_op jit(solution)/shard_map/last/pallas_call | solution.py:359
  67.9 0.9 %last.5.refs_7_ = f32[16,32,256]{2,1,0:T(8,128)S(1)} custom-call(f32[3552,256]{1,0:T(8,128)S(1)} %get-tuple-element.21.refs_0_.refs_5_, f32[3584,128]{1,0:T(8,128)S(1)} %get-tuple-element.22.refs_1_, f32[1,256,256]{2,1,0:T(8,128)S(1)} %copy-done.1, f32[2,1,32,256]{3,2,1,0:T(8,128)S(1)} %copy-done.2, f32[2,1,32,256]{3,2,1,0:T(8,128)S(1)} %copy-done.3), custom_call_target="tpu_custom_call" | custom-call | tf_op jit(solution)/shard_map/last/pallas_call | solution.py:359
  68.8 0.9 %last.4.refs_6_ = f32[16,32,256]{2,1,0:T(8,128)S(1)} custom-call(f32[3552,256]{1,0:T(8,128)S(1)} %get-tuple-element.21.refs_0_.refs_5_, f32[3584,128]{1,0:T(8,128)S(1)} %get-tuple-element.22.refs_1_, f32[1,256,256]{2,1,0:T(8,128)S(1)} %copy-done.1, f32[2,1,32,256]{3,2,1,0:T(8,128)S(1)} %copy-done.2, f32[2,1,32,256]{3,2,1,0:T(8,128)S(1)} %copy-done.3), custom_call_target="tpu_custom_call" | custom-call | tf_op jit(solution)/shard_map/last/pallas_call | solution.py:359
  69.7 0.0 collective-permute-done.10
  69.7 4.4 %combine.1 = (f32[64,32,256]{2,1,0:T(8,128)}, f32[64,32,256]{2,1,0:T(8,128)}, f32[64,32,256]{2,1,0:T(8,128)}) custom-call(f32[8,128]{1,0:T(8,128)S(1)} %add.29.refs_0_, f32[64,32,256]{2,1,0:T(8,128)S(1)} %copy-done, f32[3552,256]{1,0:T(8,128)S(1)} %get-tuple-element.18.refs_2_, f32[3552,256]{1,0:T(8,128)S(1)} %get-tuple-element.19.refs_3_, ...), custom_call_target="tpu_custom_call" | custom-call | tf_op jit(solution)/shard_map/combine/pallas_call | solution.py:371
  (8 shorter events, 0.1 us)
Async XLA Ops:
  2.4 25.5 %collective-permute-start.1 = (f32[5,32,256]{2,1,0:T(8,128)}, f32[5,32,256]{2,1,0:T(8,128)S(1)}, u32[]{:S(2)}, u32[]{:S(2)}) collective-permute-start(f32[5,32,256]{2,1,0:T(8,128)} %get-tuple-element.25), channel_id=1, source_target_pairs={{0,24},{8,0},{16,8},{24,16},{1,25},{9,1},{17,9},{25,17},{2,26},{10... | collective-permute-start | bytes 491528 | tf_op jit(solution)/shard_map/ppermute | solution.py:285
  6.3 21.6 %collective-permute-start = (f32[5,32,256]{2,1,0:T(8,128)}, f32[5,32,256]{2,1,0:T(8,128)S(1)}, u32[]{:S(2)}, u32[]{:S(2)}) collective-permute-start(f32[5,32,256]{2,1,0:T(8,128)} %get-tuple-element.26), channel_id=1, source_target_pairs={{0,8},{8,16},{16,24},{24,0},{1,9},{9,17},{17,25},{25,1},{2,10},{10... | collective-permute-start | bytes 491528 | tf_op jit(solution)/shard_map/ppermute | solution.py:285
  8.4 9.4 %collective-permute-start.2 = (f32[5,64,256]{2,1,0:T(8,128)}, f32[5,64,256]{2,1,0:T(8,128)S(1)}, u32[]{:S(2)}, u32[]{:S(2)}) collective-permute-start(f32[5,64,256]{2,1,0:T(8,128)} %bitcast.6), channel_id=1, source_target_pairs={{0,1},{1,2},{2,3},{3,4},{4,5},{5,6},{6,7},{7,0},{8,9},{9,10},{10,1... | collective-permute-start | bytes 983048 | tf_op jit(solution)/shard_map/ppermute | solution.py:285
  9.2 15.3 %copy-start = (f32[64,32,256]{2,1,0:T(8,128)S(1)}, f32[64,32,256]{2,1,0:T(8,128)}, u32[]{:S(2)}) copy-start(f32[64,32,256]{2,1,0:T(8,128)} %refs_1_.3) | copy-start | bytes 6291460
  9.2 15.3 %copy-start.1 = (f32[1,256,256]{2,1,0:T(8,128)S(1)}, f32[1,256,256]{2,1,0:T(8,128)}, u32[]{:S(2)}) copy-start(f32[1,256,256]{2,1,0:T(8,128)} %refs_2_.9) | copy-start | bytes 786436
  9.2 15.3 %copy-start.2 = (f32[2,1,32,256]{3,2,1,0:T(8,128)S(1)}, f32[2,1,32,256]{3,2,1,0:T(8,128)}, u32[]{:S(2)}) copy-start(f32[2,1,32,256]{3,2,1,0:T(8,128)} %refs_3_.9) | copy-start | bytes 196612
  9.2 15.3 %copy-start.3 = (f32[2,1,32,256]{3,2,1,0:T(8,128)S(1)}, f32[2,1,32,256]{3,2,1,0:T(8,128)}, u32[]{:S(2)}) copy-start(f32[2,1,32,256]{3,2,1,0:T(8,128)} %refs_4_.7) | copy-start | bytes 196612
  9.2 8.6 %collective-permute-start.3 = (f32[5,64,256]{2,1,0:T(8,128)}, f32[5,64,256]{2,1,0:T(8,128)S(1)}, u32[]{:S(2)}, u32[]{:S(2)}) collective-permute-start(f32[5,64,256]{2,1,0:T(8,128)} %bitcast.5), channel_id=1, source_target_pairs={{0,7},{1,0},{2,1},{3,2},{4,3},{5,4},{6,5},{7,6},{8,15},{9,8},{10,9... | collective-permute-start | bytes 983048 | tf_op jit(solution)/shard_map/ppermute | solution.py:285
  15.2 0.7 copy-start.4
  18.5 11.0 %collective-permute-start.5 = (f32[8,4,256]{2,1,0:T(4,128)}, f32[8,4,256]{2,1,0:T(4,128)S(1)}, u32[]{:S(2)}, u32[]{:S(2)}) collective-permute-start(f32[8,4,256]{2,1,0:T(4,128)} %get-tuple-element.27), channel_id=1, source_target_pairs={{0,24},{8,0},{16,8},{24,16},{1,25},{9,1},{17,9},{25,17},{2,26},{10... | collective-permute-start | bytes 98312 | tf_op jit(solution)/shard_map/ppermute | solution.py:285
  21.4 8.1 %collective-permute-start.4 = (f32[8,4,256]{2,1,0:T(4,128)}, f32[8,4,256]{2,1,0:T(4,128)S(1)}, u32[]{:S(2)}, u32[]{:S(2)}) collective-permute-start(f32[8,4,256]{2,1,0:T(4,128)} %get-tuple-element.28), channel_id=1, source_target_pairs={{0,8},{8,16},{16,24},{24,0},{1,9},{9,17},{17,25},{25,1},{2,10},{10... | collective-permute-start | bytes 98312 | tf_op jit(solution)/shard_map/ppermute | solution.py:285
  50.6 3.6 %collective-permute-start.6 = (f32[8,128]{1,0:T(8,128)S(1)}, f32[8,128]{1,0:T(8,128)S(1)}, u32[]{:S(2)}, u32[]{:S(2)}) collective-permute-start(f32[8,128]{1,0:T(8,128)S(1)} %get-tuple-element.17), channel_id=1, source_target_pairs={{0,8},{8,0},{16,24},{24,16},{1,9},{9,1},{17,25},{25,17},{2,10},{10... | collective-permute-start | bytes 12296 | tf_op jit(solution)/shard_map/ppermute | solution.py:302
  54.3 3.6 %collective-permute-start.7 = (f32[8,128]{1,0:T(8,128)S(1)}, f32[8,128]{1,0:T(8,128)S(1)}, u32[]{:S(2)}, u32[]{:S(2)}) collective-permute-start(f32[8,128]{1,0:T(8,128)S(1)} %add.25), channel_id=1, source_target_pairs={{0,16},{8,24},{16,0},{24,8},{1,17},{9,25},{17,1},{25,9},{2,18},{10... | collective-permute-start | bytes 12296 | tf_op jit(solution)/shard_map/ppermute | solution.py:302
  57.9 1.2 %collective-permute-start.8 = (f32[8,128]{1,0:T(8,128)S(1)}, f32[8,128]{1,0:T(8,128)S(1)}, u32[]{:S(2)}, u32[]{:S(2)}) collective-permute-start(f32[8,128]{1,0:T(8,128)S(1)} %add.26), channel_id=1, source_target_pairs={{0,1},{1,0},{2,3},{3,2},{4,5},{5,4},{6,7},{7,6},{8,9},{9,8},{10,11... | collective-permute-start | bytes 12296 | tf_op jit(solution)/shard_map/ppermute | solution.py:302
  59.1 3.8 %collective-permute-start.9 = (f32[8,128]{1,0:T(8,128)S(1)}, f32[8,128]{1,0:T(8,128)S(1)}, u32[]{:S(2)}, u32[]{:S(2)}) collective-permute-start(f32[8,128]{1,0:T(8,128)S(1)} %add.27), channel_id=1, source_target_pairs={{0,2},{1,3},{2,0},{3,1},{4,6},{5,7},{6,4},{7,5},{8,10},{9,11},{10,... | collective-permute-start | bytes 12296 | tf_op jit(solution)/shard_map/ppermute | solution.py:302
  62.8 6.9 %collective-permute-start.10 = (f32[8,128]{1,0:T(8,128)S(1)}, f32[8,128]{1,0:T(8,128)S(1)}, u32[]{:S(2)}, u32[]{:S(2)}) collective-permute-start(f32[8,128]{1,0:T(8,128)S(1)} %add.28), channel_id=1, source_target_pairs={{0,4},{1,5},{2,6},{3,7},{4,0},{5,1},{6,2},{7,3},{8,12},{9,13},{10,... | collective-permute-start | bytes 12296 | tf_op jit(solution)/shard_map/ppermute | solution.py:302
where the time goes:
time: 74.5 us; the launch traced here: 74.1 us
  Pallas kernels  34.1 us (46%)
  starting transfers between devices  19.4 us (26%)
  local copies, waits for them, and re-layouts  10 us (13%)
  waiting for transfers between devices  6.46 us (9%)
  other arithmetic  3.37 us (5%)
  between operations  0.82 us (1%)
    pallas_call x1, Pallas kernels, per_device(): pl.pallas_call(lambda *refs: chain_kernel(stride, *refs), out_shape=(wide...  21.1 us
    ppermute x6, starting transfers between devices, neighbour(): lax.ppermute(value, axis, [(i, (i + offset) % count) for i in range(count)])  10.4 us
    ppermute x5, starting transfers between devices, total_over(): lax.ppermute(value, axis, [(i, i ^ hop) for i in range(count)])  8.94 us
    ppermute x5, waiting for transfers between devices, total_over(): lax.ppermute(value, axis, [(i, i ^ hop) for i in range(count)])  6.44 us
    pallas_call x1, Pallas kernels, per_device(): pl.pallas_call(lambda *refs: combine_kernel(stride, chunk, pieces, *refs)...  4.39 us
    pallas_call x4, Pallas kernels, per_device(): pl.pallas_call(lambda *refs, k=k: last_kernel(stride, k * step, *refs), o...  3.64 us
    pallas_call x1, Pallas kernels, per_device(): pl.pallas_call(lambda *refs: own_kernel(stride, *refs), out_shape=(wide,...  3.29 us
    unnamed x12, local copies, waits for them, and re-layouts  2.31 us
  transfers between devices with their start and end apart: 11, of which 4 were waited for; matrix products, arithmetic and copies ran while one was open for 15% of the time, Pallas kernels for 12%

commit v1 on v0

--- a/solution.py
+++ b/solution.py
@@ -4,6 +4,7 @@
 from jax.experimental import pallas as pl
 from jax.experimental.pallas import tpu as pltpu
 from jax.sharding import PartitionSpec as P
+
 
 F32 = jnp.float32
 BF16 = jnp.bfloat16
@@ -12,7 +13,6 @@
 PAD = 8
 NT = (((1,), (1,)), ((), ()))
 NN = (((1,), (0,)), ((), ()))
-TN = (((0,), (0,)), ((), ()))
 WHOLE = pl.BlockSpec(memory_space=pltpu.VMEM)
 GRANT = pltpu.CompilerParams(vmem_limit_bytes=16 << 20)
 
@@ -70,7 +70,7 @@
     along_x = jnp.where(lane < quarter, ahead_x, behind_x)
     along_y = jnp.where(lane < 3 * quarter, ahead_y, behind_y)
     picked = jnp.where(lane < 2 * quarter, along_x, along_y)
-    level = lax.rem(lane, quarter).astype(F32)
+    level = lax.rem(lane, quarter)
     return jnp.where(level < limit, picked, 0.0)
 
 
@@ -82,6 +82,65 @@
     beside = beside + pltpu.roll(here, rows - 1, 0) + pltpu.roll(here, 1, 0)
     beside = beside + pltpu.roll(here, width - 1, 1) + pltpu.roll(here, 1, 1)
     return DIAGONAL * here - beside
+
+
+def pack_kernel(source, block, low_x, high_x, low_y, high_y, arrived):
+    cells_x, cells_y, _ = block.shape
+    step = cells_x // arrived.shape[0]
+    parts = [pl.ds(i * step, step) for i in range(arrived.shape[0])]
+    copies = [pltpu.make_async_copy(source.at[p], block.at[p], arrived.at[i]) for i, p in enumerate(parts)]
+    for copy in copies:
+        copy.start()
+    for copy, part in zip(copies, parts):
+        copy.wait()
+        for j in range(DEPTH):
+            low_y[j, part] = block[part, j]
+            high_y[j, part] = block[part, cells_y - DEPTH + j]
+    low_x[...] = block[pl.ds(0, DEPTH)]
+    high_x[...] = block[pl.ds(cells_x - DEPTH, DEPTH)]
+
+
+def corner_kernel(low_y, high_y, low_x, high_x):
+    near = DEPTH - 1
+    cells_x = low_y.shape[1]
+    for ref, first in ((low_x, 0), (high_x, cells_x - near)):
+        at = pl.ds(first, near)
+        ref[pl.ds(0, near)] = low_y[pl.ds(1, near), at]
+        ref[pl.ds(near, near)] = high_y[pl.ds(0, near), at]
+
+
+def table_kernel(stride, cells_x, cells_y, ranks, limit, rows, arrived):
+    length_x, length_y = ranks.shape[2], ranks.shape[3]
+    begin = lax.axis_index("gx") * cells_x
+    parts = (
+        (lax.rem(begin - PAD + length_x, length_x), 0, PAD),
+        (begin, PAD, cells_x),
+        (lax.rem(begin + cells_x, length_x), PAD + cells_x, PAD),
+    )
+    copies = [
+        pltpu.make_async_copy(
+            ranks.at[e, 0, pl.ds(pl.multiple_of(source, 8), size)],
+            rows.at[e, pl.ds(target, size)],
+            arrived.at[e, k],
+        )
+        for e in range(2)
+        for k, (source, target, size) in enumerate(parts)
+    ]
+    for copy in copies:
+        copy.start()
+    for copy in copies:
+        copy.wait()
+    turn = lax.rem(PAD + length_y - lax.axis_index("gy") * cells_y, length_y)
+    tall = rows.shape[1]
+    here = [pltpu.roll(pltpu.roll(rows[e], turn, 1), tall - PAD + DEPTH, 0) for e in range(2)]
+    kinds = (here[0], pltpu.roll(here[0], 1, 0), here[1], pltpu.roll(here[1], 1, 1))
+    shape = (tall, limit.shape[1])
+    kind = lax.broadcasted_iota(jnp.int32, shape, 1) // (shape[1] // 4)
+    for y in range(PAD - DEPTH + 1, PAD + cells_y + DEPTH - 1):
+        column = [jnp.broadcast_to(k[:, y : y + 1], shape) for k in kinds]
+        along_x = jnp.where(kind == 0, column[0], column[1])
+        along_y = jnp.where(kind == 2, column[2], column[3])
+        limit[pl.ds(y, tall, stride=stride)] = jnp.where(kind < 2, along_x, along_y)
 
 
 def own_kernel(stride, block, inverse, left, right, diag_out, coef_out):
@@ -138,8 +197,8 @@
 
 
 def chain_kernel(
-    stride, diag_in, coef_in, low_x, high_x, limits, block, inverse, left, right,
-    first, coef, first_image, second, second_image, limit, sums,
+    stride, diag_in, coef_in, low_x, high_x, limit, block, inverse, left, right,
+    first, coef, first_image, second, second_image, sums,
 ):
     cells_x, cells_y, width = block.shape
     square, narrow = inward(inverse, left, right)
@@ -162,18 +221,6 @@
                     first[pl.ds(at, 1)] = diag[row : row + 1]
                     coef[pl.ds(at, 1)] = coefs[row : row + 1]
 
-    kinds = limits.shape[0]
-    lane = lax.broadcasted_iota(jnp.int32, (kinds, coef.shape[1]), 1)
-    kind = lax.broadcasted_iota(jnp.int32, (kinds, coef.shape[1]), 0)
-    spread = jnp.where(lane // (coef.shape[1] // 4) == kind, 1.0, 0.0).astype(BF16)
-
-    def spread_limits(i, carry):
-        at = pl.multiple_of(i * 128, 128)
-        limit[pl.ds(at, 128)] = dot(limits[:, pl.ds(at, 128)], spread, TN)
-        return carry
-
-    lax.fori_loop(0, limits.shape[1] // 128, spread_limits, 0)
-
     def slabs(begin, end, most, work):
         step = largest_divisor(end - begin, most)
 
@@ -206,13 +253,13 @@
 
     last = 2 * DEPTH + cells_x
     body, count = slabs(1, last - 1, 9, couple(first))
-    lax.fori_loop(0, count, body, 0)
+    lax.fori_loop(0, count, body, 0, unroll=True)
     body, count = slabs(2, last - 2, 9, image_and_project)
-    lax.fori_loop(0, count, body, 0)
+    lax.fori_loop(0, count, body, 0, unroll=True)
     body, count = slabs(3, last - 3, 9, couple(second))
-    lax.fori_loop(0, count, body, 0)
+    lax.fori_loop(0, count, body, 0, unroll=True)
     body, count = slabs(4, last - 4, 9, last_image)
-    lax.fori_loop(0, count, body, 0)
+    lax.fori_loop(0, count, body, 0, unroll=True)
 
     def fold(value):
         return jnp.sum(value.reshape(cells_y // 8, 8, width), 0)
@@ -249,9 +296,8 @@
 
 
 def combine_kernel(stride, step, pieces, sums, block, z_ref, w_ref, u_ref, v_ref, *rest):
-    y_refs, (solution_out, gap_out, precond_out) = rest[:pieces], rest[pieces:]
-    i = pl.program_id(0)
-    cells_y = block.shape[1]
+    y_refs, outs, buffers, sent = rest[:pieces], rest[pieces : pieces + 3], rest[pieces + 3 : pieces + 6], rest[-1]
+    cells_x, cells_y, width = block.shape
     rz, zw, ru, wu, uv = (sums[pl.ds(k, 1), pl.ds(0, 128)] for k in range(5))
     alpha = rz / zw
     rz_next = alpha * (alpha * wu - ru)
@@ -259,21 +305,40 @@
     grown = 1.0 + ratio
     curve = grown * (grown * zw - 2.0 * alpha * wu) + alpha * alpha * uv
     alpha_next = rz_next / curve
-    s = jnp.concatenate([alpha + alpha_next * grown] * (block.shape[2] // 128), 1)
-    t = jnp.concatenate([alpha * alpha_next] * (block.shape[2] // 128), 1)
-
-    def work(y_ref):
+    s = jnp.concatenate([alpha + alpha_next * grown] * (width // 128), 1)
+    t = jnp.concatenate([alpha * alpha_next] * (width // 128), 1)
+
+    def copies(chunk):
+        part = pl.ds(chunk * step, step)
+        return [
+            pltpu.make_async_copy(buffer.at[part], out.at[part], sent.at[k, chunk])
+            for k, (buffer, out) in enumerate(zip(buffers, outs))
+        ]
+
+    per = cells_x // pieces // step
+
+    def work(i, carry, k):
+        chunk = k * per + i
         for j in range(step):
-            x = i * step + j
+            x = chunk * step + j
             at = pl.ds(pl.multiple_of((x + DEPTH) * stride + PAD, 8), cells_y)
             z0, w0, u0, v0 = z_ref[at], w_ref[at], u_ref[at], v_ref[at]
-            solution_out[j] = s * z0 - t * u0
-            gap_out[j] = (block[j] - s * w0) + t * v0
-            precond_out[j] = (z0 - s * u0) + t * y_ref[lax.rem(x, y_ref.shape[0])]
-
-    per = y_refs[0].shape[0] // step
+            buffers[0][x] = s * z0 - t * u0
+            buffers[1][x] = (block[x] - s * w0) + t * v0
+            buffers[2][x] = (z0 - s * u0) + t * y_refs[k][i * step + j]
+        for copy in copies(chunk):
+            copy.start()
+        return carry
+
     for k in range(pieces):
-        pl.when(lax.div(i, per) == k)(lambda k=k: work(y_refs[k]))
+        lax.fori_loop(0, per, lambda i, carry, k=k: work(i, carry, k), 0)
+
+    def finish(chunk, carry):
+        for copy in copies(chunk):
+            copy.wait()
+        return carry
+
+    lax.fori_loop(0, cells_x // step, finish, 0)
 
 
 def resident(*values):
@@ -283,14 +348,6 @@
 def neighbour(value, axis, offset):
     count = lax.axis_size(axis)
     return lax.ppermute(value, axis, [(i, (i + offset) % count) for i in range(count)])
-
-
-def wrapped(table, axis, begin, size, before, after):
-    length = table.shape[axis]
-    head = lax.slice_in_dim(table, length - before, length, axis=axis)
-    tail = lax.slice_in_dim(table, 0, after, axis=axis)
-    whole = jnp.concatenate([head, table, tail], axis)
-    return lax.dynamic_slice_in_dim(whole, begin, size + before + after, axis)
 
 
 def total_over(value, axis):
@@ -299,85 +356,97 @@
         return lax.psum(value, axis)
     hop = 1
     while hop < count:
-        value = value + lax.ppermute(value, axis, [(i, i ^ hop) for i in range(count)])
+        moved = lax.ppermute(value, axis, [(i, i ^ hop) for i in range(count)])
+        value = value + moved
         hop *= 2
     return value
+
+
+def call(kernel, out_shape, inputs, specs=None, **kwargs):
+    return pl.pallas_call(
+        kernel, out_shape=out_shape, in_specs=specs or [WHOLE] * len(inputs), compiler_params=GRANT, **kwargs
+    )(*inputs)
 
 
 def per_device(right_side, block_inverse, basis_left, basis_right, ranks):
     cells_x, cells_y, width = right_side.shape
     stride = cells_y + 2 * PAD
     lines = (cells_x + 2 * DEPTH) * stride
-    padded = -(-lines // 128) * 128
+    tall = cells_x + 2 * PAD
     rank4 = 4 * basis_left.shape[2]
-    weights = (block_inverse, basis_left, basis_right)
+    near = DEPTH - 1
+    weights = resident(block_inverse, basis_left, basis_right)
     wide = pltpu.VMEM((lines, width), F32)
     slim = pltpu.VMEM((lines, rank4), F32)
-
-    low_y = neighbour(jnp.transpose(right_side[:, cells_y - DEPTH :], (1, 0, 2)), "gy", 1)
-    high_y = neighbour(jnp.transpose(right_side[:, :DEPTH], (1, 0, 2)), "gy", -1)
-    low_x = neighbour(right_side[cells_x - DEPTH :], "gx", 1)
-    high_x = neighbour(right_side[:DEPTH], "gx", -1)
-
-    diag, coef = pl.pallas_call(
-        lambda *refs: own_kernel(stride, *refs),
-        out_shape=(wide, slim), in_specs=[WHOLE] * 4, out_specs=(WHOLE,) * 2, name="own", compiler_params=GRANT,
-    )(*resident(right_side, *weights))
-
-    table = wrapped(ranks[:, 0], 1, lax.axis_index("gx") * cells_x, cells_x, DEPTH + 1, DEPTH)
-    table = wrapped(table, 2, lax.axis_index("gy") * cells_y, cells_y, PAD + 1, PAD)
-    limits = jnp.stack([table[0, 1:, 1:], table[0, :-1, 1:], table[1, 1:, 1:], table[1, 1:, :-1]])
-    limits = jnp.pad(limits.reshape(4, lines).astype(F32), ((0, 4), (0, padded - lines))).astype(BF16)
-
-    near = DEPTH - 1
-    corners = jnp.concatenate([low_y[1:], high_y[:near]], 0)
-    corner_low = neighbour(corners[:, cells_x - near :], "gx", 1)
-    corner_high = neighbour(corners[:, :near], "gx", -1)
-
-    diag, coef = pl.pallas_call(
-        lambda *refs: side_kernel(stride, *refs),
-        out_shape=(wide, slim), in_specs=[WHOLE] * 9, out_specs=(WHOLE,) * 2,
-        input_output_aliases={0: 0, 1: 1}, name="side", compiler_params=GRANT,
+    edge_x = pltpu.VMEM((DEPTH, cells_y, width), F32)
+    edge_y = pltpu.VMEM((DEPTH, cells_x, width), F32)
+    corner = pltpu.VMEM((2 * near, near, width), F32)
+
+    anywhere = pl.BlockSpec(memory_space=pltpu.HBM)
+    block, out_x, in_x, out_y, in_y = call(
+        pack_kernel, (pltpu.VMEM(right_side.shape, F32), edge_x, edge_x, edge_y, edge_y), (pltpu.with_memory_space_constraint(right_side, pltpu.HBM),),
+        [anywhere], out_specs=(WHOLE,) * 5,
+        scratch_shapes=[pltpu.SemaphoreType.DMA((cells_x // largest_divisor(cells_x, 8),))],
+    )
+    (block,) = resident(block)
+    low_y = neighbour(in_y, "gy", 1)
+    high_y = neighbour(out_y, "gy", -1)
+    low_x = neighbour(in_x, "gx", 1)
+    high_x = neighbour(out_x, "gx", -1)
+
+    diag, coef = call(lambda *refs: own_kernel(stride, *refs), (wide, slim), (block, *weights), out_specs=(WHOLE,) * 2)
+    limit = call(
+        lambda *refs: table_kernel(stride, cells_x, cells_y, *refs),
+        pltpu.VMEM((tall * stride, rank4), jnp.int32), (ranks,), [pl.BlockSpec(memory_space=pl.ANY)],
+        out_specs=WHOLE,
+        scratch_shapes=[pltpu.VMEM((2, tall, ranks.shape[3]), jnp.int32), pltpu.SemaphoreType.DMA((2, 3))],
+    )
+
+    corners = call(corner_kernel, (corner, corner), resident(low_y, high_y), out_specs=(WHOLE,) * 2)
+    corner_low = neighbour(corners[1], "gx", 1)
+    corner_high = neighbour(corners[0], "gx", -1)
+
+    diag, coef = call(
+        lambda *refs: side_kernel(stride, *refs), (wide, slim),
+        (*resident(diag, coef, low_x, high_x, low_y, high_y), *weights), out_specs=(WHOLE,) * 2,
+        input_output_aliases={0: 0, 1: 1},
         scratch_shapes=[pltpu.VMEM((width // 128 + 1, cells_x * PAD, 128), F32)],
-    )(*resident(diag, coef, low_x, high_x, low_y, high_y, *weights))
-
-    first, _, first_image, second, second_image, limit, sums = pl.pallas_call(
+    )
+
+    first, _, first_image, second, second_image, sums = call(
         lambda *refs: chain_kernel(stride, *refs),
-        out_shape=(
-            wide, slim, wide, wide, wide,
-            pltpu.VMEM((padded, rank4), F32), pltpu.VMEM((8, 128), F32),
-        ),
-        in_specs=[WHOLE] * 9, out_specs=(WHOLE,) * 7,
-        input_output_aliases={0: 0, 1: 1}, name="chain", compiler_params=GRANT,
-    )(*resident(diag, coef, corner_low, corner_high, limits, right_side, *weights))
+        (wide, slim, wide, wide, wide, pltpu.VMEM((8, 128), F32)),
+        (*resident(diag, coef, corner_low, corner_high, limit), block, *weights), out_specs=(WHOLE,) * 6,
+        input_output_aliases={0: 0, 1: 1},
+    )
 
     sums = total_over(total_over(sums, "gx"), "gy")
 
     pieces = 4 if cells_x % 4 == 0 else 1
     step = cells_x // pieces
     last = [
-        pl.pallas_call(
+        call(
             lambda *refs, k=k: last_kernel(stride, k * step, *refs),
-            out_shape=pltpu.VMEM((step, cells_y, width), F32),
-            in_specs=[WHOLE] * 5, out_specs=WHOLE,
-            scratch_shapes=[pltpu.VMEM(((step + 2) * stride, rank4), F32)], name="last", compiler_params=GRANT,
-        )(*resident(second_image, limit, *weights))
+            pltpu.VMEM((step, cells_y, width), F32), (*resident(second_image, limit), *weights), out_specs=WHOLE,
+            scratch_shapes=[pltpu.VMEM(((step + 2) * stride, rank4), F32)],
+        )
         for k in range(pieces)
     ]
 
-    chunk = largest_divisor(step, 8)
-    tile = pl.BlockSpec((chunk, cells_y, width), lambda i: (i, 0, 0))
+    chunk = largest_divisor(step, 4)
     out = jax.ShapeDtypeStruct((cells_x, cells_y, width), F32)
-    return pl.pallas_call(
-        lambda *refs: combine_kernel(stride, chunk, pieces, *refs),
-        grid=(cells_x // chunk,),
-        out_shape=(out,) * 3,
-        in_specs=[WHOLE, tile] + [WHOLE] * (4 + pieces), out_specs=(tile,) * 3, name="combine", compiler_params=GRANT,
-    )(*resident(sums), right_side, *resident(first, first_image, second, second_image, *last))
+    return call(
+        lambda *refs: combine_kernel(stride, chunk, pieces, *refs), (out,) * 3,
+        (*resident(sums), block, *resident(first, first_image, second, second_image, *last)),
+        out_specs=(anywhere,) * 3,
+        scratch_shapes=[pltpu.VMEM((cells_x, cells_y, width), F32)] * 3
+        + [pltpu.SemaphoreType.DMA((3, cells_x // chunk))],
+    )
 
 
 def solution(mesh):
     placed = (P("gx", "gy", None), P(), P(), P(), P())
+
     return jax.shard_map(
         per_device,
         mesh=mesh,

time: 74.5 us -> 55.6 us (0.75)
  local copies, waits for them, and re-layouts: 10 us -> 0.02 us
  Pallas kernels: 34.1 us -> 25.3 us
  waiting for transfers between devices: 6.46 us -> 10.7 us
  other arithmetic: 3.37 us -> 0.02 us
  starting transfers between devices: 19.4 us -> 18.4 us
    pallas_call x8 -> x11, Pallas kernels: 34.1 us -> 25.3 us  [call(): pl.pallas_call(kernel, out_shape=out_shape, in_specs=specs or [WHOLE] * l...]
    slice x9 -> x0, local copies, waits for them, and re-layouts: 5.29 us -> none  [the longest x1 1.73 us: per_device(): high_x = neighbour(right_side[:DEPTH], 'gx', -1)]
    ppermute x6, waiting for transfers between devices: 0.02 us -> 3.13 us  [neighbour(): lax.ppermute(value, axis, [(i, (i + offset) % count) for i in range(count)])]
    concatenate x3 -> x0, other arithmetic: 2.7 us -> none  [the longest x2 2.07 us: wrapped(): whole = jnp.concatenate([head, table, tail], axis)]
    unnamed x12 -> x8, local copies, waits for them, and re-layouts: 2.31 us -> 0.02 us
    convert_element_type x1 -> x0, local copies, waits for them, and re-layouts: 1.64 us -> none  [per_device(): limits.reshape(4, lines).astype(F32)]
    ppermute x5, starting transfers between devices: 8.94 us -> 7.72 us  [total_over(): moved = lax.ppermute(value, axis, [(i, i ^ hop) for i in range(count)])]
    ppermute x5, waiting for transfers between devices: 6.44 us -> 7.56 us  [total_over(): moved = lax.ppermute(value, axis, [(i, i ^ hop) for i in range(count)])]
  transfers between devices with their start and end apart: 11 -> 11, of which waited for: 4 -> 6; matrix products, arithmetic and copies ran while one was open for 15% -> 0% of each run, Pallas kernels for 12% -> 20%
where the time goes in v1:
time: 55.6 us; the launch traced here: 55.4 us
  Pallas kernels  25.3 us (46%)
  starting transfers between devices  18.4 us (33%)
  waiting for transfers between devices  10.7 us (19%)
  between operations  0.95 us (2%)
    pallas_call x11, Pallas kernels, call(): pl.pallas_call(kernel, out_shape=out_shape, in_specs=specs or [WHOLE] * l...  25.3 us
    ppermute x6, starting transfers between devices, neighbour(): lax.ppermute(value, axis, [(i, (i + offset) % count) for i in range(count)])  10.7 us
    ppermute x5, starting transfers between devices, total_over(): moved = lax.ppermute(value, axis, [(i, i ^ hop) for i in range(count)])  7.72 us
    ppermute x5, waiting for transfers between devices, total_over(): moved = lax.ppermute(value, axis, [(i, i ^ hop) for i in range(count)])  7.56 us
    ppermute x6, waiting for transfers between devices, neighbour(): lax.ppermute(value, axis, [(i, (i + offset) % count) for i in range(count)])  3.13 us
  transfers between devices with their start and end apart: 11, of which 6 were waited for; matrix products, arithmetic and copies ran while one was open for 0% of the time, Pallas kernels for 20%

profile of v1, /device:TPU:0, one launch (start us, length us, event | category | flops | bytes accessed | tf_op | source)
XLA Modules:
  0.0 55.4 jit_solution(12522226294932603646)
XLA Ops:
  0.6 0.0 copy-start.3
  0.6 1.7 %shard_map.76 = (f32[64,32,256]{2,1,0:T(8,128)S(1)}, f32[5,32,256]{2,1,0:T(8,128)S(1)}, f32[5,32,256]{2,1,0:T(8,128)S(1)}, f32[5,64,256]{2,1,0:T(8,128)S(1)}, f32[5,64,256]{2,1,0:T(8,128)S(1)}) custom-call(f32[64,32,256]{2,1,0:T(8,128)} %source.1), custom_call_target="tpu_custom_call" | custom-call | tf_op jit(solution)/shard_map/pallas_call | solution.py:366
  2.3 0.0 copy-start
  2.3 0.0 copy-start.1
  2.3 0.0 copy-start.2
  2.4 0.5 collective-permute-start.2
  2.9 4.1 %collective-permute-start.3 = (f32[5,64,256]{2,1,0:T(8,128)S(1)}, f32[5,64,256]{2,1,0:T(8,128)S(1)}, u32[]{:S(2)}, u32[]{:S(2)}) collective-permute-start(f32[5,64,256]{2,1,0:T(8,128)S(1)} %get-tuple-element.25), channel_id=1, source_target_pairs={{0,7},{1,0},{2,1},{3,2},{4,3},{5,4},{6,5},{7,6},{8,15},{9,8},{10,9... | collective-permute-start | bytes 983048 | tf_op jit(solution)/shard_map/ppermute | solution.py:350
  7.0 1.9 %collective-permute-start = (f32[5,32,256]{2,1,0:T(8,128)S(1)}, f32[5,32,256]{2,1,0:T(8,128)S(1)}, u32[]{:S(2)}, u32[]{:S(2)}) collective-permute-start(f32[5,32,256]{2,1,0:T(8,128)S(1)} %get-tuple-element.22), channel_id=1, source_target_pairs={{0,8},{8,16},{16,24},{24,0},{1,9},{9,17},{17,25},{25,1},{2,10},{10... | collective-permute-start | bytes 491528 | tf_op jit(solution)/shard_map/ppermute | solution.py:350
  8.9 1.0 %collective-permute-start.1 = (f32[5,32,256]{2,1,0:T(8,128)S(1)}, f32[5,32,256]{2,1,0:T(8,128)S(1)}, u32[]{:S(2)}, u32[]{:S(2)}) collective-permute-start(f32[5,32,256]{2,1,0:T(8,128)S(1)} %get-tuple-element.23), channel_id=1, source_target_pairs={{0,24},{8,0},{16,8},{24,16},{1,25},{9,1},{17,9},{25,17},{2,26},{10... | collective-permute-start | bytes 491528 | tf_op jit(solution)/shard_map/ppermute | solution.py:350
  9.9 2.7 %collective-permute-done.2.refs_4_.low_y = f32[5,64,256]{2,1,0:T(8,128)S(1)} collective-permute-done((f32[5,64,256]{2,1,0:T(8,128)S(1)}, f32[5,64,256]{2,1,0:T(8,128)S(1)}, u32[]{:S(2)}, u32[]{:S(2)}) %collective-permute-start.2) | collective-permute-done | bytes 327712 | tf_op jit(solution)/shard_map/ppermute | solution.py:350
  12.6 0.4 collective-permute-done.3.refs_5_.high_y
  13.0 2.1 %collective-permute-start.4 = (f32[8,4,256]{2,1,0:T(4,128)S(1)}, f32[8,4,256]{2,1,0:T(4,128)S(1)}, u32[]{:S(2)}, u32[]{:S(2)}) collective-permute-start(f32[8,4,256]{2,1,0:T(4,128)S(1)} %get-tuple-element.28), channel_id=1, source_target_pairs={{0,8},{8,16},{16,24},{24,0},{1,9},{9,17},{17,25},{25,1},{2,10},{10... | collective-permute-start | bytes 98312 | tf_op jit(solution)/shard_map/ppermute | solution.py:350
  15.2 1.0 %collective-permute-start.5 = (f32[8,4,256]{2,1,0:T(4,128)S(1)}, f32[8,4,256]{2,1,0:T(4,128)S(1)}, u32[]{:S(2)}, u32[]{:S(2)}) collective-permute-start(f32[8,4,256]{2,1,0:T(4,128)S(1)} %get-tuple-element.29), channel_id=1, source_target_pairs={{0,24},{8,0},{16,8},{24,16},{1,25},{9,1},{17,9},{25,17},{2,26},{10... | collective-permute-start | bytes 98312 | tf_op jit(solution)/shard_map/ppermute | solution.py:350
  16.2 0.0 copy-done.3
  16.2 2.3 %shard_map.80.refs_4_.refs_1_ = s32[3840,128]{1,0:T(8,128)S(1)} custom-call(s32[2,1,256,256]{3,2,1,0:T(8,128)S(1)} %copy-done.3), custom_call_target="tpu_custom_call" | custom-call | tf_op jit(solution)/shard_map/pallas_call | solution.py:366
  18.5 0.0 copy-done
  18.5 0.0 copy-done.1
  18.5 0.0 copy-done.2
  18.5 3.3 %shard_map.77 = (f32[3552,256]{1,0:T(8,128)S(1)}, f32[3552,128]{1,0:T(8,128)S(1)}) custom-call(f32[64,32,256]{2,1,0:T(8,128)S(1)} %get-tuple-element.19.refs_0_.refs_5_.refs_1_, f32[1,256,256]{2,1,0:T(8,128)S(1)} %copy-done, f32[2,1,32,256]{3,2,1,0:T(8,128)S(1)} %copy-done.1, f32[2,1,32,256]{3,2,1,0:T(8,128)S(1)} %copy-done.2), custom_call_target="tpu_custom_call" | custom-call | tf_op jit(solution)/shard_map/pallas_call | solution.py:366
  21.8 0.0 collective-permute-done.refs_2_
  21.9 0.0 collective-permute-done.1.refs_3_
  21.9 1.6 %shard_map.78 = (f32[3552,256]{1,0:T(8,128)S(1)}, f32[3552,128]{1,0:T(8,128)S(1)}) custom-call(f32[3552,256]{1,0:T(8,128)S(1)} %get-tuple-element.20.refs_0_, f32[3552,128]{1,0:T(8,128)S(1)} %get-tuple-element.21.refs_1_, f32[5,32,256]{2,1,0:T(8,128)S(1)} %collective-permute-done.refs_2_, ...), custom_call_target="tpu_custom_call", output_to_operand_aliasing={{0}: (0, {}), {1}: (1, {})} | custom-call | tf_op jit(solution)/shard_map/pallas_call | solution.py:366
  23.5 0.0 collective-permute-done.4.refs_2_
  23.5 0.0 collective-permute-done.5.refs_3_
  23.5 9.6 %shard_map.81 = (f32[3552,256]{1,0:T(8,128)S(1)}, f32[3552,128]{1,0:T(8,128)S(1)}, f32[3552,256]{1,0:T(8,128)S(1)}, f32[3552,256]{1,0:T(8,128)S(1)}, f32[3552,256]{1,0:T(8,128)S(1)}, /*index=5*/f32[8,128]{1,0:T(8,128)S(1)}) custom-call(f32[3552,256]{1,0:T(8,128)S(1)} %get-tuple-element.26.refs_0_, ...), custom_call_target="tpu_custom_call", output_to_operand_aliasing={{0}: (0, {}), {1}: (1, {})} | custom-call | tf_op jit(solution)/shard_map/pallas_call | solution.py:366
  33.1 1.0 %collective-permute-start.6 = (f32[8,128]{1,0:T(8,128)S(1)}, f32[8,128]{1,0:T(8,128)S(1)}, u32[]{:S(2)}, u32[]{:S(2)}) collective-permute-start(f32[8,128]{1,0:T(8,128)S(1)} %get-tuple-element.30), channel_id=1, source_target_pairs={{0,8},{8,0},{16,24},{24,16},{1,9},{9,1},{17,25},{25,17},{2,10},{10... | collective-permute-start | bytes 12296 | tf_op jit(solution)/shard_map/ppermute | solution.py:359
  34.1 2.6 %collective-permute-done.6 = f32[8,128]{1,0:T(8,128)S(1)} collective-permute-done((f32[8,128]{1,0:T(8,128)S(1)}, f32[8,128]{1,0:T(8,128)S(1)}, u32[]{:S(2)}, u32[]{:S(2)}) %collective-permute-start.6) | collective-permute-done | bytes 4128 | tf_op jit(solution)/shard_map/ppermute | solution.py:359
  36.7 1.9 %collective-permute-start.7 = (f32[8,128]{1,0:T(8,128)S(1)}, f32[8,128]{1,0:T(8,128)S(1)}, u32[]{:S(2)}, u32[]{:S(2)}) collective-permute-start(f32[8,128]{1,0:T(8,128)S(1)} %add.15), channel_id=1, source_target_pairs={{0,16},{8,24},{16,0},{24,8},{1,17},{9,25},{17,1},{25,9},{2,18},{10... | collective-permute-start | bytes 12296 | tf_op jit(solution)/shard_map/ppermute | solution.py:359
  38.6 1.7 %collective-permute-done.7 = f32[8,128]{1,0:T(8,128)S(1)} collective-permute-done((f32[8,128]{1,0:T(8,128)S(1)}, f32[8,128]{1,0:T(8,128)S(1)}, u32[]{:S(2)}, u32[]{:S(2)}) %collective-permute-start.7) | collective-permute-done | bytes 4128 | tf_op jit(solution)/shard_map/ppermute | solution.py:359
  40.3 0.0 collective-permute-start.8
  40.3 1.2 %collective-permute-done.8 = f32[8,128]{1,0:T(8,128)S(1)} collective-permute-done((f32[8,128]{1,0:T(8,128)S(1)}, f32[8,128]{1,0:T(8,128)S(1)}, u32[]{:S(2)}, u32[]{:S(2)}) %collective-permute-start.8) | collective-permute-done | bytes 4128 | tf_op jit(solution)/shard_map/ppermute | solution.py:359
  41.5 1.6 %collective-permute-start.9 = (f32[8,128]{1,0:T(8,128)S(1)}, f32[8,128]{1,0:T(8,128)S(1)}, u32[]{:S(2)}, u32[]{:S(2)}) collective-permute-start(f32[8,128]{1,0:T(8,128)S(1)} %add.17), channel_id=1, source_target_pairs={{0,2},{1,3},{2,0},{3,1},{4,6},{5,7},{6,4},{7,5},{8,10},{9,11},{10,... | collective-permute-start | bytes 12296 | tf_op jit(solution)/shard_map/ppermute | solution.py:359
  43.0 2.1 %collective-permute-done.9 = f32[8,128]{1,0:T(8,128)S(1)} collective-permute-done((f32[8,128]{1,0:T(8,128)S(1)}, f32[8,128]{1,0:T(8,128)S(1)}, u32[]{:S(2)}, u32[]{:S(2)}) %collective-permute-start.9) | collective-permute-done | bytes 4128 | tf_op jit(solution)/shard_map/ppermute | solution.py:359
  45.1 3.3 %collective-permute-start.10 = (f32[8,128]{1,0:T(8,128)S(1)}, f32[8,128]{1,0:T(8,128)S(1)}, u32[]{:S(2)}, u32[]{:S(2)}) collective-permute-start(f32[8,128]{1,0:T(8,128)S(1)} %add.18), channel_id=1, source_target_pairs={{0,4},{1,5},{2,6},{3,7},{4,0},{5,1},{6,2},{7,3},{8,12},{9,13},{10,... | collective-permute-start | bytes 12296 | tf_op jit(solution)/shard_map/ppermute | solution.py:359
  48.4 0.9 %shard_map.85.refs_9_ = f32[16,32,256]{2,1,0:T(8,128)S(1)} custom-call(f32[3552,256]{1,0:T(8,128)S(1)} %get-tuple-element.34.refs_0_.refs_5_, s32[3840,128]{1,0:T(8,128)S(1)} %shard_map.80.refs_4_.refs_1_, f32[1,256,256]{2,1,0:T(8,128)S(1)} %copy-done, f32[2,1,32,256]{3,2,1,0:T(8,128)S(1)} %copy-done.1, f32[2,1,32,256]{3,2,1,0:T(8,128)S(1)} %copy-done.2), custom_call_target="tpu_custom_call" | custom-call | tf_op jit(solution)/shard_map/pallas_call | solution.py:366
  49.3 0.9 %shard_map.84.refs_8_ = f32[16,32,256]{2,1,0:T(8,128)S(1)} custom-call(f32[3552,256]{1,0:T(8,128)S(1)} %get-tuple-element.34.refs_0_.refs_5_, s32[3840,128]{1,0:T(8,128)S(1)} %shard_map.80.refs_4_.refs_1_, f32[1,256,256]{2,1,0:T(8,128)S(1)} %copy-done, f32[2,1,32,256]{3,2,1,0:T(8,128)S(1)} %copy-done.1, f32[2,1,32,256]{3,2,1,0:T(8,128)S(1)} %copy-done.2), custom_call_target="tpu_custom_call" | custom-call | tf_op jit(solution)/shard_map/pallas_call | solution.py:366
  50.2 0.9 %shard_map.83.refs_7_ = f32[16,32,256]{2,1,0:T(8,128)S(1)} custom-call(f32[3552,256]{1,0:T(8,128)S(1)} %get-tuple-element.34.refs_0_.refs_5_, s32[3840,128]{1,0:T(8,128)S(1)} %shard_map.80.refs_4_.refs_1_, f32[1,256,256]{2,1,0:T(8,128)S(1)} %copy-done, f32[2,1,32,256]{3,2,1,0:T(8,128)S(1)} %copy-done.1, f32[2,1,32,256]{3,2,1,0:T(8,128)S(1)} %copy-done.2), custom_call_target="tpu_custom_call" | custom-call | tf_op jit(solution)/shard_map/pallas_call | solution.py:366
  51.2 0.9 %shard_map.82.refs_6_ = f32[16,32,256]{2,1,0:T(8,128)S(1)} custom-call(f32[3552,256]{1,0:T(8,128)S(1)} %get-tuple-element.34.refs_0_.refs_5_, s32[3840,128]{1,0:T(8,128)S(1)} %shard_map.80.refs_4_.refs_1_, f32[1,256,256]{2,1,0:T(8,128)S(1)} %copy-done, f32[2,1,32,256]{3,2,1,0:T(8,128)S(1)} %copy-done.1, f32[2,1,32,256]{3,2,1,0:T(8,128)S(1)} %copy-done.2), custom_call_target="tpu_custom_call" | custom-call | tf_op jit(solution)/shard_map/pallas_call | solution.py:366
  52.1 0.0 collective-permute-done.10
  52.2 3.1 %shard_map.86 = (f32[64,32,256]{2,1,0:T(8,128)}, f32[64,32,256]{2,1,0:T(8,128)}, f32[64,32,256]{2,1,0:T(8,128)}) custom-call(f32[8,128]{1,0:T(8,128)S(1)} %add.19.refs_0_, f32[64,32,256]{2,1,0:T(8,128)S(1)} %get-tuple-element.19.refs_0_.refs_5_.refs_1_, f32[3552,256]{1,0:T(8,128)S(1)} %get-tuple-element.31.refs_2_, ...), custom_call_target="tpu_custom_call" | custom-call | tf_op jit(solution)/shard_map/pallas_call | solution.py:366
  (6 shorter events, 0.0 us)
Async XLA Ops:
  0.6 15.5 %copy-start.3 = (s32[2,1,256,256]{3,2,1,0:T(8,128)S(1)}, s32[2,1,256,256]{3,2,1,0:T(8,128)}, u32[]{:S(2)}) copy-start(s32[2,1,256,256]{3,2,1,0:T(8,128)} %refs_0_.1) | copy-start | bytes 1572868
  2.3 16.2 %copy-start = (f32[1,256,256]{2,1,0:T(8,128)S(1)}, f32[1,256,256]{2,1,0:T(8,128)}, u32[]{:S(2)}) copy-start(f32[1,256,256]{2,1,0:T(8,128)} %refs_2_.9) | copy-start | bytes 786436
  2.3 16.2 %copy-start.1 = (f32[2,1,32,256]{3,2,1,0:T(8,128)S(1)}, f32[2,1,32,256]{3,2,1,0:T(8,128)}, u32[]{:S(2)}) copy-start(f32[2,1,32,256]{3,2,1,0:T(8,128)} %refs_3_.9) | copy-start | bytes 196612
  2.3 16.2 %copy-start.2 = (f32[2,1,32,256]{3,2,1,0:T(8,128)S(1)}, f32[2,1,32,256]{3,2,1,0:T(8,128)}, u32[]{:S(2)}) copy-start(f32[2,1,32,256]{3,2,1,0:T(8,128)} %refs_4_.7) | copy-start | bytes 196612
  2.4 10.2 %collective-permute-start.2 = (f32[5,64,256]{2,1,0:T(8,128)S(1)}, f32[5,64,256]{2,1,0:T(8,128)S(1)}, u32[]{:S(2)}, u32[]{:S(2)}) collective-permute-start(f32[5,64,256]{2,1,0:T(8,128)S(1)} %get-tuple-element.24), channel_id=1, source_target_pairs={{0,1},{1,2},{2,3},{3,4},{4,5},{5,6},{6,7},{7,0},{8,9},{9,10},{10,1... | collective-permute-start | bytes 983048 | tf_op jit(solution)/shard_map/ppermute | solution.py:350
  2.9 10.1 %collective-permute-start.3 = (f32[5,64,256]{2,1,0:T(8,128)S(1)}, f32[5,64,256]{2,1,0:T(8,128)S(1)}, u32[]{:S(2)}, u32[]{:S(2)}) collective-permute-start(f32[5,64,256]{2,1,0:T(8,128)S(1)} %get-tuple-element.25), channel_id=1, source_target_pairs={{0,7},{1,0},{2,1},{3,2},{4,3},{5,4},{6,5},{7,6},{8,15},{9,8},{10,9... | collective-permute-start | bytes 983048 | tf_op jit(solution)/shard_map/ppermute | solution.py:350
  7.0 14.9 %collective-permute-start = (f32[5,32,256]{2,1,0:T(8,128)S(1)}, f32[5,32,256]{2,1,0:T(8,128)S(1)}, u32[]{:S(2)}, u32[]{:S(2)}) collective-permute-start(f32[5,32,256]{2,1,0:T(8,128)S(1)} %get-tuple-element.22), channel_id=1, source_target_pairs={{0,8},{8,16},{16,24},{24,0},{1,9},{9,17},{17,25},{25,1},{2,10},{10... | collective-permute-start | bytes 491528 | tf_op jit(solution)/shard_map/ppermute | solution.py:350
  8.9 12.9 %collective-permute-start.1 = (f32[5,32,256]{2,1,0:T(8,128)S(1)}, f32[5,32,256]{2,1,0:T(8,128)S(1)}, u32[]{:S(2)}, u32[]{:S(2)}) collective-permute-start(f32[5,32,256]{2,1,0:T(8,128)S(1)} %get-tuple-element.23), channel_id=1, source_target_pairs={{0,24},{8,0},{16,8},{24,16},{1,25},{9,1},{17,9},{25,17},{2,26},{10... | collective-permute-start | bytes 491528 | tf_op jit(solution)/shard_map/ppermute | solution.py:350
  13.0 10.4 %collective-permute-start.4 = (f32[8,4,256]{2,1,0:T(4,128)S(1)}, f32[8,4,256]{2,1,0:T(4,128)S(1)}, u32[]{:S(2)}, u32[]{:S(2)}) collective-permute-start(f32[8,4,256]{2,1,0:T(4,128)S(1)} %get-tuple-element.28), channel_id=1, source_target_pairs={{0,8},{8,16},{16,24},{24,0},{1,9},{9,17},{17,25},{25,1},{2,10},{10... | collective-permute-start | bytes 98312 | tf_op jit(solution)/shard_map/ppermute | solution.py:350
  15.2 8.4 %collective-permute-start.5 = (f32[8,4,256]{2,1,0:T(4,128)S(1)}, f32[8,4,256]{2,1,0:T(4,128)S(1)}, u32[]{:S(2)}, u32[]{:S(2)}) collective-permute-start(f32[8,4,256]{2,1,0:T(4,128)S(1)} %get-tuple-element.29), channel_id=1, source_target_pairs={{0,24},{8,0},{16,8},{24,16},{1,25},{9,1},{17,9},{25,17},{2,26},{10... | collective-permute-start | bytes 98312 | tf_op jit(solution)/shard_map/ppermute | solution.py:350
  33.1 3.6 %collective-permute-start.6 = (f32[8,128]{1,0:T(8,128)S(1)}, f32[8,128]{1,0:T(8,128)S(1)}, u32[]{:S(2)}, u32[]{:S(2)}) collective-permute-start(f32[8,128]{1,0:T(8,128)S(1)} %get-tuple-element.30), channel_id=1, source_target_pairs={{0,8},{8,0},{16,24},{24,16},{1,9},{9,1},{17,25},{25,17},{2,10},{10... | collective-permute-start | bytes 12296 | tf_op jit(solution)/shard_map/ppermute | solution.py:359
  36.7 3.6 %collective-permute-start.7 = (f32[8,128]{1,0:T(8,128)S(1)}, f32[8,128]{1,0:T(8,128)S(1)}, u32[]{:S(2)}, u32[]{:S(2)}) collective-permute-start(f32[8,128]{1,0:T(8,128)S(1)} %add.15), channel_id=1, source_target_pairs={{0,16},{8,24},{16,0},{24,8},{1,17},{9,25},{17,1},{25,9},{2,18},{10... | collective-permute-start | bytes 12296 | tf_op jit(solution)/shard_map/ppermute | solution.py:359
  40.3 1.2 %collective-permute-start.8 = (f32[8,128]{1,0:T(8,128)S(1)}, f32[8,128]{1,0:T(8,128)S(1)}, u32[]{:S(2)}, u32[]{:S(2)}) collective-permute-start(f32[8,128]{1,0:T(8,128)S(1)} %add.16), channel_id=1, source_target_pairs={{0,1},{1,0},{2,3},{3,2},{4,5},{5,4},{6,7},{7,6},{8,9},{9,8},{10,11... | collective-permute-start | bytes 12296 | tf_op jit(solution)/shard_map/ppermute | solution.py:359
  41.5 3.6 %collective-permute-start.9 = (f32[8,128]{1,0:T(8,128)S(1)}, f32[8,128]{1,0:T(8,128)S(1)}, u32[]{:S(2)}, u32[]{:S(2)}) collective-permute-start(f32[8,128]{1,0:T(8,128)S(1)} %add.17), channel_id=1, source_target_pairs={{0,2},{1,3},{2,0},{3,1},{4,6},{5,7},{6,4},{7,5},{8,10},{9,11},{10,... | collective-permute-start | bytes 12296 | tf_op jit(solution)/shard_map/ppermute | solution.py:359
  45.1 7.0 %collective-permute-start.10 = (f32[8,128]{1,0:T(8,128)S(1)}, f32[8,128]{1,0:T(8,128)S(1)}, u32[]{:S(2)}, u32[]{:S(2)}) collective-permute-start(f32[8,128]{1,0:T(8,128)S(1)} %add.18), channel_id=1, source_target_pairs={{0,4},{1,5},{2,6},{3,7},{4,0},{5,1},{6,2},{7,3},{8,12},{9,13},{10,... | collective-permute-start | bytes 12296 | tf_op jit(solution)/shard_map/ppermute | solution.py:359

commit v2 on v1

--- a/solution.py
+++ b/solution.py
@@ -159,7 +159,7 @@
             coef_out[pl.ds(at, cells_y)] = coef[j * cells_y : (j + 1) * cells_y]
         return carry
 
-    lax.fori_loop(0, cells_x // step, body, 0)
+    lax.fori_loop(0, cells_x // step, body, 0, unroll=True)
 
 
 def side_kernel(stride, diag_in, coef_in, low_x, high_x, low_y, high_y, inverse, left, right, diag_out, coef_out, turned):
@@ -198,7 +198,7 @@
 
 def chain_kernel(
     stride, diag_in, coef_in, low_x, high_x, limit, block, inverse, left, right,
-    first, coef, first_image, second, second_image, sums,
+    first, coef, first_image, second, sums,
 ):
     cells_x, cells_y, width = block.shape
     square, narrow = inward(inverse, left, right)
@@ -221,82 +221,85 @@
                     first[pl.ds(at, 1)] = diag[row : row + 1]
                     coef[pl.ds(at, 1)] = coefs[row : row + 1]
 
-    def slabs(begin, end, most, work):
+    def slabs(begin, end, most):
         step = largest_divisor(end - begin, most)
-
-        def body(i, carry):
-            return work(pl.multiple_of((begin + i * step) * stride, 8), step * stride, carry)
-
-        return body, (end - begin) // step
-
-    def couple(ref):
-        def work(start, rows, carry):
-            at = pl.ds(start, rows)
-            picked = gathered(coef, start, rows, stride, limit[at])
-            ref[at] = ref[at] + coupling_part(picked, factors)
-            return carry
-
-        return work
-
-    def image_and_project(start, rows, carry):
-        at = pl.ds(start, rows)
-        image = operated(first, start, rows, stride)
+        return [(x, step) for x in range(begin, end, step)]
+
+    def inside(value, x, step):
+        value = value.reshape(step, stride, value.shape[1])[:, PAD : PAD + cells_y]
+        return value[max(DEPTH - x, 0) : max(DEPTH + cells_x - x, 0)]
+
+    def owned(x, step):
+        return max(x - DEPTH, 0), min(x + step - DEPTH, cells_x)
+
+    def summed(value):
+        return jnp.sum(value.reshape(-1, 8, width), 0)
+
+    totals = [jnp.zeros((8, width), F32)] * 6
+    last = 2 * DEPTH + cells_x
+    for x, step in slabs(1, last - 1, 9):
+        at = pl.ds(x * stride, step * stride)
+        picked = gathered(coef, x * stride, step * stride, stride, limit[at])
+        first[at] = first[at] + coupling_part(picked, factors)
+    for x, step in slabs(2, last - 2, 9):
+        at = pl.ds(x * stride, step * stride)
+        image = operated(first, x * stride, step * stride, stride)
         first_image[at] = image
         high, low = halves(image)
         second[at] = diagonal_part(high, low, square)
         coef[at] = coefficients(high, low, narrow)
-        return carry
-
-    def last_image(start, rows, carry):
-        second_image[pl.ds(start, rows)] = operated(second, start, rows, stride)
-        return carry
-
-    last = 2 * DEPTH + cells_x
-    body, count = slabs(1, last - 1, 9, couple(first))
-    lax.fori_loop(0, count, body, 0, unroll=True)
-    body, count = slabs(2, last - 2, 9, image_and_project)
-    lax.fori_loop(0, count, body, 0, unroll=True)
-    body, count = slabs(3, last - 3, 9, couple(second))
-    lax.fori_loop(0, count, body, 0, unroll=True)
-    body, count = slabs(4, last - 4, 9, last_image)
-    lax.fori_loop(0, count, body, 0, unroll=True)
-
-    def fold(value):
-        return jnp.sum(value.reshape(cells_y // 8, 8, width), 0)
-
-    def products(x, carry):
-        at = pl.ds(pl.multiple_of((x + DEPTH) * stride + PAD, 8), cells_y)
-        rhs = block[x]
-        z0, w0, u0, v0 = first[at], first_image[at], second[at], second_image[at]
-        terms = (rhs * z0, z0 * w0, rhs * u0, w0 * u0, u0 * v0)
-        return tuple(c + fold(t) for c, t in zip(carry, terms))
-
-    zero = jnp.zeros((8, width), F32)
-    parts = lax.fori_loop(0, cells_x, products, (zero,) * 5)
-    rows = [jnp.sum(jnp.sum(p, 0, keepdims=True), 1, keepdims=True) for p in parts]
+        begin, end = owned(x, step)
+        if begin < end:
+            field = inside(first[at], x, step)
+            totals[0] += summed(block[pl.ds(begin, end - begin)] * field)
+            totals[1] += summed(inside(image, x, step) * field)
+    for x, step in slabs(3, last - 3, 9):
+        at = pl.ds(x * stride, step * stride)
+        picked = gathered(coef, x * stride, step * stride, stride, limit[at])
+        field = second[at] + coupling_part(picked, factors)
+        second[at] = field
+        begin, end = owned(x, step)
+        if begin < end:
+            field = inside(field, x, step)
+            totals[2] += summed(block[pl.ds(begin, end - begin)] * field)
+            totals[3] += summed(inside(first_image[at], x, step) * field)
+            totals[4] += summed(field * field)
+    for x, step in slabs(DEPTH, DEPTH + cells_x, 8):
+        start, rows = x * stride, step * stride
+        here = second[pl.ds(start, rows)]
+        beside = second[pl.ds(start + stride, rows)] + pltpu.roll(here, rows - 1, 0) + pltpu.roll(here, width - 1, 1)
+        totals[5] += summed(inside(here * beside, x, step))
+    totals = totals[:4] + [DIAGONAL * totals[4] - 2.0 * totals[5]]
+    rows = [jnp.sum(jnp.sum(p, 0, keepdims=True), 1, keepdims=True) for p in totals]
     for i, row in enumerate(rows):
         sums[pl.ds(i, 1)] = jnp.broadcast_to(row, (1, sums.shape[1]))
     sums[pl.ds(5, 3)] = jnp.zeros((3, sums.shape[1]), F32)
 
 
-def last_kernel(stride, begin, field, limit, inverse, left, right, out, coef):
+def last_kernel(stride, begin, field, limit, inverse, left, right, image_out, out, image, coef):
     step, cells_y, width = out.shape
     square, narrow = inward(inverse, left, right)
     factors = outward(left, right)
     start = (begin + DEPTH) * stride
-    high, low = halves(field[pl.ds(start - stride, (step + 2) * stride)])
-    coef[...] = coefficients(high, low, narrow)
+    part = largest_divisor(step + 2, 9)
+    for x in range(0, step + 2, part):
+        at = pl.ds(x * stride, part * stride)
+        value = operated(field, start + (x - 1) * stride, part * stride, stride)
+        image[at] = value
+        coef[at] = coefficients(*halves(value), narrow)
     picked = gathered(coef, stride, step * stride, stride, limit[pl.ds(start, step * stride)])
     picked = picked.reshape(step, stride, picked.shape[1])[:, PAD : PAD + cells_y]
-    rows = field[pl.ds(start, step * stride)].reshape(step, stride, width)[:, PAD : PAD + cells_y]
+    rows = image[pl.ds(stride, step * stride)].reshape(step, stride, width)[:, PAD : PAD + cells_y]
+    image_out[...] = rows
     high, low = halves(rows.reshape(step * cells_y, width))
     total = diagonal_part(high, low, square)
     total = total + coupling_part(picked.reshape(step * cells_y, picked.shape[2]), factors)
     out[...] = total.reshape(step, cells_y, width)
 
 
-def combine_kernel(stride, step, pieces, sums, block, z_ref, w_ref, u_ref, v_ref, *rest):
-    y_refs, outs, buffers, sent = rest[:pieces], rest[pieces : pieces + 3], rest[pieces + 3 : pieces + 6], rest[-1]
+def combine_kernel(stride, step, pieces, sums, block, z_ref, w_ref, u_ref, *rest):
+    v_refs, y_refs, rest = rest[0 : 2 * pieces : 2], rest[1 : 2 * pieces : 2], rest[2 * pieces :]
+    outs, buffers, sent = rest[:3], rest[3:6], rest[6]
     cells_x, cells_y, width = block.shape
     rz, zw, ru, wu, uv = (sums[pl.ds(k, 1), pl.ds(0, 128)] for k in range(5))
     alpha = rz / zw
@@ -322,16 +325,16 @@
         for j in range(step):
             x = chunk * step + j
             at = pl.ds(pl.multiple_of((x + DEPTH) * stride + PAD, 8), cells_y)
-            z0, w0, u0, v0 = z_ref[at], w_ref[at], u_ref[at], v_ref[at]
+            z0, w0, u0 = z_ref[at], w_ref[at], u_ref[at]
             buffers[0][x] = s * z0 - t * u0
-            buffers[1][x] = (block[x] - s * w0) + t * v0
+            buffers[1][x] = (block[x] - s * w0) + t * v_refs[k][i * step + j]
             buffers[2][x] = (z0 - s * u0) + t * y_refs[k][i * step + j]
         for copy in copies(chunk):
             copy.start()
         return carry
 
     for k in range(pieces):
-        lax.fori_loop(0, per, lambda i, carry, k=k: work(i, carry, k), 0)
+        lax.fori_loop(0, per, lambda i, carry, k=k: work(i, carry, k), 0, unroll=True)
 
     def finish(chunk, carry):
         for copy in copies(chunk):
@@ -413,10 +416,10 @@
         scratch_shapes=[pltpu.VMEM((width // 128 + 1, cells_x * PAD, 128), F32)],
     )
 
-    first, _, first_image, second, second_image, sums = call(
+    first, _, first_image, second, sums = call(
         lambda *refs: chain_kernel(stride, *refs),
-        (wide, slim, wide, wide, wide, pltpu.VMEM((8, 128), F32)),
-        (*resident(diag, coef, corner_low, corner_high, limit), block, *weights), out_specs=(WHOLE,) * 6,
+        (wide, slim, wide, wide, pltpu.VMEM((8, 128), F32)),
+        (*resident(diag, coef, corner_low, corner_high, limit), block, *weights), out_specs=(WHOLE,) * 5,
         input_output_aliases={0: 0, 1: 1},
     )
 
@@ -424,20 +427,22 @@
 
     pieces = 4 if cells_x % 4 == 0 else 1
     step = cells_x // pieces
+    piece = pltpu.VMEM((step, cells_y, width), F32)
     last = [
-        call(
-            lambda *refs, k=k: last_kernel(stride, k * step, *refs),
-            pltpu.VMEM((step, cells_y, width), F32), (*resident(second_image, limit), *weights), out_specs=WHOLE,
-            scratch_shapes=[pltpu.VMEM(((step + 2) * stride, rank4), F32)],
+        array
+        for k in range(pieces)
+        for array in call(
+            lambda *refs, k=k: last_kernel(stride, k * step, *refs), (piece, piece),
+            (*resident(second, limit), *weights), out_specs=(WHOLE,) * 2,
+            scratch_shapes=[pltpu.VMEM(((step + 2) * stride, n), F32) for n in (width, rank4)],
         )
-        for k in range(pieces)
     ]
 
-    chunk = largest_divisor(step, 4)
+    chunk = largest_divisor(step, 8)
     out = jax.ShapeDtypeStruct((cells_x, cells_y, width), F32)
     return call(
         lambda *refs: combine_kernel(stride, chunk, pieces, *refs), (out,) * 3,
-        (*resident(sums), block, *resident(first, first_image, second, second_image, *last)),
+        (*resident(sums), block, *resident(first, first_image, second, *last)),
         out_specs=(anywhere,) * 3,
         scratch_shapes=[pltpu.VMEM((cells_x, cells_y, width), F32)] * 3
         + [pltpu.SemaphoreType.DMA((3, cells_x // chunk))],

time: 55.6 us -> 53.2 us (0.957)
  Pallas kernels: 25.3 us -> 23 us
    pallas_call x11, Pallas kernels: 25.3 us -> 23 us  [call(): pl.pallas_call(kernel, out_shape=out_shape, in_specs=specs or [WHOLE] * l...]
where the time goes in v2:
time: 53.2 us; the launch traced here: 53.1 us
  Pallas kernels  23 us (43%)
  starting transfers between devices  18.5 us (35%)
  waiting for transfers between devices  10.6 us (20%)
  between operations  0.96 us (2%)
    pallas_call x11, Pallas kernels, call(): pl.pallas_call(kernel, out_shape=out_shape, in_specs=specs or [WHOLE] * l...  23 us
    ppermute x6, starting transfers between devices, neighbour(): lax.ppermute(value, axis, [(i, (i + offset) % count) for i in range(count)])  10.7 us
    ppermute x5, starting transfers between devices, total_over(): moved = lax.ppermute(value, axis, [(i, i ^ hop) for i in range(count)])  7.81 us
    ppermute x5, waiting for transfers between devices, total_over(): moved = lax.ppermute(value, axis, [(i, i ^ hop) for i in range(count)])  7.48 us
    ppermute x6, waiting for transfers between devices, neighbour(): lax.ppermute(value, axis, [(i, (i + offset) % count) for i in range(count)])  3.13 us
  transfers between devices with their start and end apart: 11, of which 6 were waited for; matrix products, arithmetic and copies ran while one was open for 0% of the time, Pallas kernels for 20%

profile of v2, /device:TPU:0, one launch (start us, length us, event | category | flops | bytes accessed | tf_op | source)
XLA Modules:
  0.0 53.1 jit_solution(7732921087426371128)
XLA Ops:
  0.6 0.0 copy-start.3
  0.6 1.7 %shard_map.76 = (f32[64,32,256]{2,1,0:T(8,128)S(1)}, f32[5,32,256]{2,1,0:T(8,128)S(1)}, f32[5,32,256]{2,1,0:T(8,128)S(1)}, f32[5,64,256]{2,1,0:T(8,128)S(1)}, f32[5,64,256]{2,1,0:T(8,128)S(1)}) custom-call(f32[64,32,256]{2,1,0:T(8,128)} %source.1), custom_call_target="tpu_custom_call" | custom-call | tf_op jit(solution)/shard_map/pallas_call | solution.py:369
  2.3 0.0 copy-start
  2.3 0.0 copy-start.1
  2.3 0.0 copy-start.2
  2.4 0.5 %collective-permute-start.2 = (f32[5,64,256]{2,1,0:T(8,128)S(1)}, f32[5,64,256]{2,1,0:T(8,128)S(1)}, u32[]{:S(2)}, u32[]{:S(2)}) collective-permute-start(f32[5,64,256]{2,1,0:T(8,128)S(1)} %get-tuple-element.31), channel_id=1, source_target_pairs={{0,1},{1,2},{2,3},{3,4},{4,5},{5,6},{6,7},{7,0},{8,9},{9,10},{10,1... | collective-permute-start | bytes 983048 | tf_op jit(solution)/shard_map/ppermute | solution.py:353
  2.9 4.1 %collective-permute-start.3 = (f32[5,64,256]{2,1,0:T(8,128)S(1)}, f32[5,64,256]{2,1,0:T(8,128)S(1)}, u32[]{:S(2)}, u32[]{:S(2)}) collective-permute-start(f32[5,64,256]{2,1,0:T(8,128)S(1)} %get-tuple-element.32), channel_id=1, source_target_pairs={{0,7},{1,0},{2,1},{3,2},{4,3},{5,4},{6,5},{7,6},{8,15},{9,8},{10,9... | collective-permute-start | bytes 983048 | tf_op jit(solution)/shard_map/ppermute | solution.py:353
  7.0 1.9 %collective-permute-start = (f32[5,32,256]{2,1,0:T(8,128)S(1)}, f32[5,32,256]{2,1,0:T(8,128)S(1)}, u32[]{:S(2)}, u32[]{:S(2)}) collective-permute-start(f32[5,32,256]{2,1,0:T(8,128)S(1)} %get-tuple-element.29), channel_id=1, source_target_pairs={{0,8},{8,16},{16,24},{24,0},{1,9},{9,17},{17,25},{25,1},{2,10},{10... | collective-permute-start | bytes 491528 | tf_op jit(solution)/shard_map/ppermute | solution.py:353
  8.9 1.0 %collective-permute-start.1 = (f32[5,32,256]{2,1,0:T(8,128)S(1)}, f32[5,32,256]{2,1,0:T(8,128)S(1)}, u32[]{:S(2)}, u32[]{:S(2)}) collective-permute-start(f32[5,32,256]{2,1,0:T(8,128)S(1)} %get-tuple-element.30), channel_id=1, source_target_pairs={{0,24},{8,0},{16,8},{24,16},{1,25},{9,1},{17,9},{25,17},{2,26},{10... | collective-permute-start | bytes 491528 | tf_op jit(solution)/shard_map/ppermute | solution.py:353
  9.9 2.7 %collective-permute-done.2.refs_4_.low_y = f32[5,64,256]{2,1,0:T(8,128)S(1)} collective-permute-done((f32[5,64,256]{2,1,0:T(8,128)S(1)}, f32[5,64,256]{2,1,0:T(8,128)S(1)}, u32[]{:S(2)}, u32[]{:S(2)}) %collective-permute-start.2) | collective-permute-done | bytes 327712 | tf_op jit(solution)/shard_map/ppermute | solution.py:353
  12.6 0.4 collective-permute-done.3.refs_5_.high_y
  13.0 2.1 %collective-permute-start.4 = (f32[8,4,256]{2,1,0:T(4,128)S(1)}, f32[8,4,256]{2,1,0:T(4,128)S(1)}, u32[]{:S(2)}, u32[]{:S(2)}) collective-permute-start(f32[8,4,256]{2,1,0:T(4,128)S(1)} %get-tuple-element.35), channel_id=1, source_target_pairs={{0,8},{8,16},{16,24},{24,0},{1,9},{9,17},{17,25},{25,1},{2,10},{10... | collective-permute-start | bytes 98312 | tf_op jit(solution)/shard_map/ppermute | solution.py:353
  15.2 1.0 %collective-permute-start.5 = (f32[8,4,256]{2,1,0:T(4,128)S(1)}, f32[8,4,256]{2,1,0:T(4,128)S(1)}, u32[]{:S(2)}, u32[]{:S(2)}) collective-permute-start(f32[8,4,256]{2,1,0:T(4,128)S(1)} %get-tuple-element.36), channel_id=1, source_target_pairs={{0,24},{8,0},{16,8},{24,16},{1,25},{9,1},{17,9},{25,17},{2,26},{10... | collective-permute-start | bytes 98312 | tf_op jit(solution)/shard_map/ppermute | solution.py:353
  16.2 0.0 copy-done.3
  16.2 2.3 %shard_map.80.refs_4_.refs_1_ = s32[3840,128]{1,0:T(8,128)S(1)} custom-call(s32[2,1,256,256]{3,2,1,0:T(8,128)S(1)} %copy-done.3), custom_call_target="tpu_custom_call" | custom-call | tf_op jit(solution)/shard_map/pallas_call | solution.py:369
  18.5 0.0 copy-done
  18.5 0.0 copy-done.1
  18.5 0.0 copy-done.2
  18.5 1.6 %shard_map.77 = (f32[3552,256]{1,0:T(8,128)S(1)}, f32[3552,128]{1,0:T(8,128)S(1)}) custom-call(f32[64,32,256]{2,1,0:T(8,128)S(1)} %get-tuple-element.26.refs_0_.refs_5_.refs_1_, f32[1,256,256]{2,1,0:T(8,128)S(1)} %copy-done, f32[2,1,32,256]{3,2,1,0:T(8,128)S(1)} %copy-done.1, f32[2,1,32,256]{3,2,1,0:T(8,128)S(1)} %copy-done.2), custom_call_target="tpu_custom_call" | custom-call | tf_op jit(solution)/shard_map/pallas_call | solution.py:369
  20.1 0.0 collective-permute-done.refs_2_
  20.1 0.0 collective-permute-done.1.refs_3_
  20.1 1.8 %shard_map.78 = (f32[3552,256]{1,0:T(8,128)S(1)}, f32[3552,128]{1,0:T(8,128)S(1)}) custom-call(f32[3552,256]{1,0:T(8,128)S(1)} %get-tuple-element.27.refs_0_, f32[3552,128]{1,0:T(8,128)S(1)} %get-tuple-element.28.refs_1_, f32[5,32,256]{2,1,0:T(8,128)S(1)} %collective-permute-done.refs_2_, ...), custom_call_target="tpu_custom_call", output_to_operand_aliasing={{0}: (0, {}), {1}: (1, {})} | custom-call | tf_op jit(solution)/shard_map/pallas_call | solution.py:369
  21.9 0.0 collective-permute-done.4.refs_2_
  21.9 0.0 collective-permute-done.5.refs_3_
  22.0 8.0 %shard_map.81 = (f32[3552,256]{1,0:T(8,128)S(1)}, f32[3552,128]{1,0:T(8,128)S(1)}, f32[3552,256]{1,0:T(8,128)S(1)}, f32[3552,256]{1,0:T(8,128)S(1)}, f32[8,128]{1,0:T(8,128)S(1)}) custom-call(f32[3552,256]{1,0:T(8,128)S(1)} %get-tuple-element.33.refs_0_, f32[3552,128]{1,0:T(8,128)S(1)} %get-tuple-element.34.refs_1_, ...), custom_call_target="tpu_custom_call", output_to_operand_aliasing={{0}: (0, {}), {1}: (1, {})} | custom-call | tf_op jit(solution)/shard_map/pallas_call | solution.py:369
  30.0 1.0 %collective-permute-start.6 = (f32[8,128]{1,0:T(8,128)S(1)}, f32[8,128]{1,0:T(8,128)S(1)}, u32[]{:S(2)}, u32[]{:S(2)}) collective-permute-start(f32[8,128]{1,0:T(8,128)S(1)} %get-tuple-element.37), channel_id=1, source_target_pairs={{0,8},{8,0},{16,24},{24,16},{1,9},{9,1},{17,25},{25,17},{2,10},{10... | collective-permute-start | bytes 12296 | tf_op jit(solution)/shard_map/ppermute | solution.py:362
  31.0 2.6 %collective-permute-done.6 = f32[8,128]{1,0:T(8,128)S(1)} collective-permute-done((f32[8,128]{1,0:T(8,128)S(1)}, f32[8,128]{1,0:T(8,128)S(1)}, u32[]{:S(2)}, u32[]{:S(2)}) %collective-permute-start.6) | collective-permute-done | bytes 4128 | tf_op jit(solution)/shard_map/ppermute | solution.py:362
  33.6 1.9 %collective-permute-start.7 = (f32[8,128]{1,0:T(8,128)S(1)}, f32[8,128]{1,0:T(8,128)S(1)}, u32[]{:S(2)}, u32[]{:S(2)}) collective-permute-start(f32[8,128]{1,0:T(8,128)S(1)} %add.15), channel_id=1, source_target_pairs={{0,16},{8,24},{16,0},{24,8},{1,17},{9,25},{17,1},{25,9},{2,18},{10... | collective-permute-start | bytes 12296 | tf_op jit(solution)/shard_map/ppermute | solution.py:362
  35.5 1.7 %collective-permute-done.7 = f32[8,128]{1,0:T(8,128)S(1)} collective-permute-done((f32[8,128]{1,0:T(8,128)S(1)}, f32[8,128]{1,0:T(8,128)S(1)}, u32[]{:S(2)}, u32[]{:S(2)}) %collective-permute-start.7) | collective-permute-done | bytes 4128 | tf_op jit(solution)/shard_map/ppermute | solution.py:362
  37.2 0.0 collective-permute-start.8
  37.2 1.2 %collective-permute-done.8 = f32[8,128]{1,0:T(8,128)S(1)} collective-permute-done((f32[8,128]{1,0:T(8,128)S(1)}, f32[8,128]{1,0:T(8,128)S(1)}, u32[]{:S(2)}, u32[]{:S(2)}) %collective-permute-start.8) | collective-permute-done | bytes 4128 | tf_op jit(solution)/shard_map/ppermute | solution.py:362
  38.4 1.6 %collective-permute-start.9 = (f32[8,128]{1,0:T(8,128)S(1)}, f32[8,128]{1,0:T(8,128)S(1)}, u32[]{:S(2)}, u32[]{:S(2)}) collective-permute-start(f32[8,128]{1,0:T(8,128)S(1)} %add.17), channel_id=1, source_target_pairs={{0,2},{1,3},{2,0},{3,1},{4,6},{5,7},{6,4},{7,5},{8,10},{9,11},{10,... | collective-permute-start | bytes 12296 | tf_op jit(solution)/shard_map/ppermute | solution.py:362
  39.9 2.0 %collective-permute-done.9 = f32[8,128]{1,0:T(8,128)S(1)} collective-permute-done((f32[8,128]{1,0:T(8,128)S(1)}, f32[8,128]{1,0:T(8,128)S(1)}, u32[]{:S(2)}, u32[]{:S(2)}) %collective-permute-start.9) | collective-permute-done | bytes 4128 | tf_op jit(solution)/shard_map/ppermute | solution.py:362
  42.0 3.3 %collective-permute-start.10 = (f32[8,128]{1,0:T(8,128)S(1)}, f32[8,128]{1,0:T(8,128)S(1)}, u32[]{:S(2)}, u32[]{:S(2)}) collective-permute-start(f32[8,128]{1,0:T(8,128)S(1)} %add.18), channel_id=1, source_target_pairs={{0,4},{1,5},{2,6},{3,7},{4,0},{5,1},{6,2},{7,3},{8,12},{9,13},{10,... | collective-permute-start | bytes 12296 | tf_op jit(solution)/shard_map/ppermute | solution.py:362
  45.3 1.2 %shard_map.85 = (f32[16,32,256]{2,1,0:T(8,128)S(1)}, f32[16,32,256]{2,1,0:T(8,128)S(1)}) custom-call(f32[3552,256]{1,0:T(8,128)S(1)} %get-tuple-element.40.refs_0_.refs_4_, s32[3840,128]{1,0:T(8,128)S(1)} %shard_map.80.refs_4_.refs_1_, f32[1,256,256]{2,1,0:T(8,128)S(1)} %copy-done, f32[2,1,32,256]{3,2,1,0:T(8,128)S(1)} %copy-done.1, ...), custom_call_target="tpu_custom_call" | custom-call | tf_op jit(solution)/shard_map/pallas_call | solution.py:369
  46.4 1.2 %shard_map.84 = (f32[16,32,256]{2,1,0:T(8,128)S(1)}, f32[16,32,256]{2,1,0:T(8,128)S(1)}) custom-call(f32[3552,256]{1,0:T(8,128)S(1)} %get-tuple-element.40.refs_0_.refs_4_, s32[3840,128]{1,0:T(8,128)S(1)} %shard_map.80.refs_4_.refs_1_, f32[1,256,256]{2,1,0:T(8,128)S(1)} %copy-done, f32[2,1,32,256]{3,2,1,0:T(8,128)S(1)} %copy-done.1, ...), custom_call_target="tpu_custom_call" | custom-call | tf_op jit(solution)/shard_map/pallas_call | solution.py:369
  47.6 1.2 %shard_map.83 = (f32[16,32,256]{2,1,0:T(8,128)S(1)}, f32[16,32,256]{2,1,0:T(8,128)S(1)}) custom-call(f32[3552,256]{1,0:T(8,128)S(1)} %get-tuple-element.40.refs_0_.refs_4_, s32[3840,128]{1,0:T(8,128)S(1)} %shard_map.80.refs_4_.refs_1_, f32[1,256,256]{2,1,0:T(8,128)S(1)} %copy-done, f32[2,1,32,256]{3,2,1,0:T(8,128)S(1)} %copy-done.1, ...), custom_call_target="tpu_custom_call" | custom-call | tf_op jit(solution)/shard_map/pallas_call | solution.py:369
  48.8 1.2 %shard_map.82 = (f32[16,32,256]{2,1,0:T(8,128)S(1)}, f32[16,32,256]{2,1,0:T(8,128)S(1)}) custom-call(f32[3552,256]{1,0:T(8,128)S(1)} %get-tuple-element.40.refs_0_.refs_4_, s32[3840,128]{1,0:T(8,128)S(1)} %shard_map.80.refs_4_.refs_1_, f32[1,256,256]{2,1,0:T(8,128)S(1)} %copy-done, f32[2,1,32,256]{3,2,1,0:T(8,128)S(1)} %copy-done.1, ...), custom_call_target="tpu_custom_call" | custom-call | tf_op jit(solution)/shard_map/pallas_call | solution.py:369
  50.0 0.0 collective-permute-done.10
  50.0 2.9 %shard_map.86 = (f32[64,32,256]{2,1,0:T(8,128)}, f32[64,32,256]{2,1,0:T(8,128)}, f32[64,32,256]{2,1,0:T(8,128)}) custom-call(f32[8,128]{1,0:T(8,128)S(1)} %add.19.refs_0_, f32[64,32,256]{2,1,0:T(8,128)S(1)} %get-tuple-element.26.refs_0_.refs_5_.refs_1_, f32[3552,256]{1,0:T(8,128)S(1)} %get-tuple-element.38.refs_2_, ...), custom_call_target="tpu_custom_call" | custom-call | tf_op jit(solution)/shard_map/pallas_call | solution.py:369
  (6 shorter events, 0.0 us)
Async XLA Ops:
  0.6 15.5 %copy-start.3 = (s32[2,1,256,256]{3,2,1,0:T(8,128)S(1)}, s32[2,1,256,256]{3,2,1,0:T(8,128)}, u32[]{:S(2)}) copy-start(s32[2,1,256,256]{3,2,1,0:T(8,128)} %refs_0_.1) | copy-start | bytes 1572868
  2.3 16.2 %copy-start = (f32[1,256,256]{2,1,0:T(8,128)S(1)}, f32[1,256,256]{2,1,0:T(8,128)}, u32[]{:S(2)}) copy-start(f32[1,256,256]{2,1,0:T(8,128)} %refs_2_.9) | copy-start | bytes 786436
  2.3 16.2 %copy-start.1 = (f32[2,1,32,256]{3,2,1,0:T(8,128)S(1)}, f32[2,1,32,256]{3,2,1,0:T(8,128)}, u32[]{:S(2)}) copy-start(f32[2,1,32,256]{3,2,1,0:T(8,128)} %refs_3_.9) | copy-start | bytes 196612
  2.3 16.2 %copy-start.2 = (f32[2,1,32,256]{3,2,1,0:T(8,128)S(1)}, f32[2,1,32,256]{3,2,1,0:T(8,128)}, u32[]{:S(2)}) copy-start(f32[2,1,32,256]{3,2,1,0:T(8,128)} %refs_4_.7) | copy-start | bytes 196612
  2.4 10.2 %collective-permute-start.2 = (f32[5,64,256]{2,1,0:T(8,128)S(1)}, f32[5,64,256]{2,1,0:T(8,128)S(1)}, u32[]{:S(2)}, u32[]{:S(2)}) collective-permute-start(f32[5,64,256]{2,1,0:T(8,128)S(1)} %get-tuple-element.31), channel_id=1, source_target_pairs={{0,1},{1,2},{2,3},{3,4},{4,5},{5,6},{6,7},{7,0},{8,9},{9,10},{10,1... | collective-permute-start | bytes 983048 | tf_op jit(solution)/shard_map/ppermute | solution.py:353
  2.9 10.1 %collective-permute-start.3 = (f32[5,64,256]{2,1,0:T(8,128)S(1)}, f32[5,64,256]{2,1,0:T(8,128)S(1)}, u32[]{:S(2)}, u32[]{:S(2)}) collective-permute-start(f32[5,64,256]{2,1,0:T(8,128)S(1)} %get-tuple-element.32), channel_id=1, source_target_pairs={{0,7},{1,0},{2,1},{3,2},{4,3},{5,4},{6,5},{7,6},{8,15},{9,8},{10,9... | collective-permute-start | bytes 983048 | tf_op jit(solution)/shard_map/ppermute | solution.py:353
  7.0 13.1 %collective-permute-start = (f32[5,32,256]{2,1,0:T(8,128)S(1)}, f32[5,32,256]{2,1,0:T(8,128)S(1)}, u32[]{:S(2)}, u32[]{:S(2)}) collective-permute-start(f32[5,32,256]{2,1,0:T(8,128)S(1)} %get-tuple-element.29), channel_id=1, source_target_pairs={{0,8},{8,16},{16,24},{24,0},{1,9},{9,17},{17,25},{25,1},{2,10},{10... | collective-permute-start | bytes 491528 | tf_op jit(solution)/shard_map/ppermute | solution.py:353
  8.9 11.2 %collective-permute-start.1 = (f32[5,32,256]{2,1,0:T(8,128)S(1)}, f32[5,32,256]{2,1,0:T(8,128)S(1)}, u32[]{:S(2)}, u32[]{:S(2)}) collective-permute-start(f32[5,32,256]{2,1,0:T(8,128)S(1)} %get-tuple-element.30), channel_id=1, source_target_pairs={{0,24},{8,0},{16,8},{24,16},{1,25},{9,1},{17,9},{25,17},{2,26},{10... | collective-permute-start | bytes 491528 | tf_op jit(solution)/shard_map/ppermute | solution.py:353
  13.0 8.9 %collective-permute-start.4 = (f32[8,4,256]{2,1,0:T(4,128)S(1)}, f32[8,4,256]{2,1,0:T(4,128)S(1)}, u32[]{:S(2)}, u32[]{:S(2)}) collective-permute-start(f32[8,4,256]{2,1,0:T(4,128)S(1)} %get-tuple-element.35), channel_id=1, source_target_pairs={{0,8},{8,16},{16,24},{24,0},{1,9},{9,17},{17,25},{25,1},{2,10},{10... | collective-permute-start | bytes 98312 | tf_op jit(solution)/shard_map/ppermute | solution.py:353
  15.2 6.8 %collective-permute-start.5 = (f32[8,4,256]{2,1,0:T(4,128)S(1)}, f32[8,4,256]{2,1,0:T(4,128)S(1)}, u32[]{:S(2)}, u32[]{:S(2)}) collective-permute-start(f32[8,4,256]{2,1,0:T(4,128)S(1)} %get-tuple-element.36), channel_id=1, source_target_pairs={{0,24},{8,0},{16,8},{24,16},{1,25},{9,1},{17,9},{25,17},{2,26},{10... | collective-permute-start | bytes 98312 | tf_op jit(solution)/shard_map/ppermute | solution.py:353
  30.0 3.6 %collective-permute-start.6 = (f32[8,128]{1,0:T(8,128)S(1)}, f32[8,128]{1,0:T(8,128)S(1)}, u32[]{:S(2)}, u32[]{:S(2)}) collective-permute-start(f32[8,128]{1,0:T(8,128)S(1)} %get-tuple-element.37), channel_id=1, source_target_pairs={{0,8},{8,0},{16,24},{24,16},{1,9},{9,1},{17,25},{25,17},{2,10},{10... | collective-permute-start | bytes 12296 | tf_op jit(solution)/shard_map/ppermute | solution.py:362
  33.6 3.6 %collective-permute-start.7 = (f32[8,128]{1,0:T(8,128)S(1)}, f32[8,128]{1,0:T(8,128)S(1)}, u32[]{:S(2)}, u32[]{:S(2)}) collective-permute-start(f32[8,128]{1,0:T(8,128)S(1)} %add.15), channel_id=1, source_target_pairs={{0,16},{8,24},{16,0},{24,8},{1,17},{9,25},{17,1},{25,9},{2,18},{10... | collective-permute-start | bytes 12296 | tf_op jit(solution)/shard_map/ppermute | solution.py:362
  37.2 1.2 %collective-permute-start.8 = (f32[8,128]{1,0:T(8,128)S(1)}, f32[8,128]{1,0:T(8,128)S(1)}, u32[]{:S(2)}, u32[]{:S(2)}) collective-permute-start(f32[8,128]{1,0:T(8,128)S(1)} %add.16), channel_id=1, source_target_pairs={{0,1},{1,0},{2,3},{3,2},{4,5},{5,4},{6,7},{7,6},{8,9},{9,8},{10,11... | collective-permute-start | bytes 12296 | tf_op jit(solution)/shard_map/ppermute | solution.py:362
  38.4 3.6 %collective-permute-start.9 = (f32[8,128]{1,0:T(8,128)S(1)}, f32[8,128]{1,0:T(8,128)S(1)}, u32[]{:S(2)}, u32[]{:S(2)}) collective-permute-start(f32[8,128]{1,0:T(8,128)S(1)} %add.17), channel_id=1, source_target_pairs={{0,2},{1,3},{2,0},{3,1},{4,6},{5,7},{6,4},{7,5},{8,10},{9,11},{10,... | collective-permute-start | bytes 12296 | tf_op jit(solution)/shard_map/ppermute | solution.py:362
  42.0 8.0 %collective-permute-start.10 = (f32[8,128]{1,0:T(8,128)S(1)}, f32[8,128]{1,0:T(8,128)S(1)}, u32[]{:S(2)}, u32[]{:S(2)}) collective-permute-start(f32[8,128]{1,0:T(8,128)S(1)} %add.18), channel_id=1, source_target_pairs={{0,4},{1,5},{2,6},{3,7},{4,0},{5,1},{6,2},{7,3},{8,12},{9,13},{10,... | collective-permute-start | bytes 12296 | tf_op jit(solution)/shard_map/ppermute | solution.py:362

commit v3 on v2

--- a/solution.py
+++ b/solution.py
@@ -357,11 +357,15 @@
     count = lax.axis_size(axis)
     if count & (count - 1):
         return lax.psum(value, axis)
-    hop = 1
+    groups, hop = [], 1
+    if count.bit_length() % 2 == 0:
+        groups, hop = [(1,)], 2
     while hop < count:
-        moved = lax.ppermute(value, axis, [(i, i ^ hop) for i in range(count)])
-        value = value + moved
-        hop *= 2
+        groups.append((2 * hop, hop, 3 * hop))
+        hop *= 4
+    for hops in groups:
+        moved = [lax.ppermute(value, axis, [(i, i ^ h) for i in range(count)]) for h in hops]
+        value = sum(moved, value)
     return value
 
 

time: 53.2 us -> 50.6 us (0.951)
  waiting for transfers between devices: 10.6 us -> 7.81 us
    ppermute x5 -> x7, waiting for transfers between devices: 7.48 us -> 4.68 us  [total_over(): lax.ppermute(value, axis, [(i, i ^ h) for i in range(count)])]
    ppermute x5 -> x7, starting transfers between devices: 7.81 us -> 7.96 us  [total_over(): lax.ppermute(value, axis, [(i, i ^ h) for i in range(count)])]
  transfers between devices with their start and end apart: 11 -> 13, of which waited for: 6 -> 6; matrix products, arithmetic and copies ran while one was open for 0% -> 0% of each run, Pallas kernels for 20% -> 21%
where the time goes in v3:
time: 50.6 us; the launch traced here: 50.4 us
  Pallas kernels  23 us (45%)
  starting transfers between devices  18.6 us (37%)
  waiting for transfers between devices  7.81 us (15%)
  between operations  0.98 us (2%)
    pallas_call x11, Pallas kernels, call(): pl.pallas_call(kernel, out_shape=out_shape, in_specs=specs or [WHOLE] * l...  23 us
    ppermute x6, starting transfers between devices, neighbour(): lax.ppermute(value, axis, [(i, (i + offset) % count) for i in range(count)])  10.7 us
    ppermute x7, starting transfers between devices, total_over(): lax.ppermute(value, axis, [(i, i ^ h) for i in range(count)])  7.96 us
    ppermute x7, waiting for transfers between devices, total_over(): lax.ppermute(value, axis, [(i, i ^ h) for i in range(count)])  4.68 us
    ppermute x6, waiting for transfers between devices, neighbour(): lax.ppermute(value, axis, [(i, (i + offset) % count) for i in range(count)])  3.13 us
  transfers between devices with their start and end apart: 13, of which 6 were waited for; matrix products, arithmetic and copies ran while one was open for 0% of the time, Pallas kernels for 21%

profile of v3, /device:TPU:0, one launch (start us, length us, event | category | flops | bytes accessed | tf_op | source)
XLA Modules:
  0.0 50.4 jit_solution(4328281418226577073)
XLA Ops:
  0.6 0.0 copy-start.3
  0.6 1.7 %shard_map.76 = (f32[64,32,256]{2,1,0:T(8,128)S(1)}, f32[5,32,256]{2,1,0:T(8,128)S(1)}, f32[5,32,256]{2,1,0:T(8,128)S(1)}, f32[5,64,256]{2,1,0:T(8,128)S(1)}, f32[5,64,256]{2,1,0:T(8,128)S(1)}) custom-call(f32[64,32,256]{2,1,0:T(8,128)} %source.1), custom_call_target="tpu_custom_call" | custom-call | tf_op jit(solution)/shard_map/pallas_call | solution.py:373
  2.3 0.0 copy-start
  2.3 0.0 copy-start.1
  2.3 0.0 copy-start.2
  2.4 0.5 %collective-permute-start.2 = (f32[5,64,256]{2,1,0:T(8,128)S(1)}, f32[5,64,256]{2,1,0:T(8,128)S(1)}, u32[]{:S(2)}, u32[]{:S(2)}) collective-permute-start(f32[5,64,256]{2,1,0:T(8,128)S(1)} %get-tuple-element.31), channel_id=1, source_target_pairs={{0,1},{1,2},{2,3},{3,4},{4,5},{5,6},{6,7},{7,0},{8,9},{9,10},{10,1... | collective-permute-start | bytes 983048 | tf_op jit(solution)/shard_map/ppermute | solution.py:353
  2.9 4.1 %collective-permute-start.3 = (f32[5,64,256]{2,1,0:T(8,128)S(1)}, f32[5,64,256]{2,1,0:T(8,128)S(1)}, u32[]{:S(2)}, u32[]{:S(2)}) collective-permute-start(f32[5,64,256]{2,1,0:T(8,128)S(1)} %get-tuple-element.32), channel_id=1, source_target_pairs={{0,7},{1,0},{2,1},{3,2},{4,3},{5,4},{6,5},{7,6},{8,15},{9,8},{10,9... | collective-permute-start | bytes 983048 | tf_op jit(solution)/shard_map/ppermute | solution.py:353
  7.0 1.9 %collective-permute-start = (f32[5,32,256]{2,1,0:T(8,128)S(1)}, f32[5,32,256]{2,1,0:T(8,128)S(1)}, u32[]{:S(2)}, u32[]{:S(2)}) collective-permute-start(f32[5,32,256]{2,1,0:T(8,128)S(1)} %get-tuple-element.29), channel_id=1, source_target_pairs={{0,8},{8,16},{16,24},{24,0},{1,9},{9,17},{17,25},{25,1},{2,10},{10... | collective-permute-start | bytes 491528 | tf_op jit(solution)/shard_map/ppermute | solution.py:353
  8.9 1.0 %collective-permute-start.1 = (f32[5,32,256]{2,1,0:T(8,128)S(1)}, f32[5,32,256]{2,1,0:T(8,128)S(1)}, u32[]{:S(2)}, u32[]{:S(2)}) collective-permute-start(f32[5,32,256]{2,1,0:T(8,128)S(1)} %get-tuple-element.30), channel_id=1, source_target_pairs={{0,24},{8,0},{16,8},{24,16},{1,25},{9,1},{17,9},{25,17},{2,26},{10... | collective-permute-start | bytes 491528 | tf_op jit(solution)/shard_map/ppermute | solution.py:353
  9.9 2.7 %collective-permute-done.2.refs_4_.low_y = f32[5,64,256]{2,1,0:T(8,128)S(1)} collective-permute-done((f32[5,64,256]{2,1,0:T(8,128)S(1)}, f32[5,64,256]{2,1,0:T(8,128)S(1)}, u32[]{:S(2)}, u32[]{:S(2)}) %collective-permute-start.2) | collective-permute-done | bytes 327712 | tf_op jit(solution)/shard_map/ppermute | solution.py:353
  12.6 0.4 collective-permute-done.3.refs_5_.high_y
  13.0 2.1 %collective-permute-start.4 = (f32[8,4,256]{2,1,0:T(4,128)S(1)}, f32[8,4,256]{2,1,0:T(4,128)S(1)}, u32[]{:S(2)}, u32[]{:S(2)}) collective-permute-start(f32[8,4,256]{2,1,0:T(4,128)S(1)} %get-tuple-element.35), channel_id=1, source_target_pairs={{0,8},{8,16},{16,24},{24,0},{1,9},{9,17},{17,25},{25,1},{2,10},{10... | collective-permute-start | bytes 98312 | tf_op jit(solution)/shard_map/ppermute | solution.py:353
  15.2 1.0 %collective-permute-start.5 = (f32[8,4,256]{2,1,0:T(4,128)S(1)}, f32[8,4,256]{2,1,0:T(4,128)S(1)}, u32[]{:S(2)}, u32[]{:S(2)}) collective-permute-start(f32[8,4,256]{2,1,0:T(4,128)S(1)} %get-tuple-element.36), channel_id=1, source_target_pairs={{0,24},{8,0},{16,8},{24,16},{1,25},{9,1},{17,9},{25,17},{2,26},{10... | collective-permute-start | bytes 98312 | tf_op jit(solution)/shard_map/ppermute | solution.py:353
  16.2 0.0 copy-done.3
  16.2 2.3 %shard_map.80.refs_4_.refs_1_ = s32[3840,128]{1,0:T(8,128)S(1)} custom-call(s32[2,1,256,256]{3,2,1,0:T(8,128)S(1)} %copy-done.3), custom_call_target="tpu_custom_call" | custom-call | tf_op jit(solution)/shard_map/pallas_call | solution.py:373
  18.5 0.0 copy-done
  18.5 0.0 copy-done.1
  18.5 0.0 copy-done.2
  18.5 1.6 %shard_map.77 = (f32[3552,256]{1,0:T(8,128)S(1)}, f32[3552,128]{1,0:T(8,128)S(1)}) custom-call(f32[64,32,256]{2,1,0:T(8,128)S(1)} %get-tuple-element.26.refs_0_.refs_5_.refs_1_, f32[1,256,256]{2,1,0:T(8,128)S(1)} %copy-done, f32[2,1,32,256]{3,2,1,0:T(8,128)S(1)} %copy-done.1, f32[2,1,32,256]{3,2,1,0:T(8,128)S(1)} %copy-done.2), custom_call_target="tpu_custom_call" | custom-call | tf_op jit(solution)/shard_map/pallas_call | solution.py:373
  20.1 0.0 collective-permute-done.refs_2_
  20.1 0.0 collective-permute-done.1.refs_3_
  20.1 1.8 %shard_map.78 = (f32[3552,256]{1,0:T(8,128)S(1)}, f32[3552,128]{1,0:T(8,128)S(1)}) custom-call(f32[3552,256]{1,0:T(8,128)S(1)} %get-tuple-element.27.refs_0_, f32[3552,128]{1,0:T(8,128)S(1)} %get-tuple-element.28.refs_1_, f32[5,32,256]{2,1,0:T(8,128)S(1)} %collective-permute-done.refs_2_, ...), custom_call_target="tpu_custom_call", output_to_operand_aliasing={{0}: (0, {}), {1}: (1, {})} | custom-call | tf_op jit(solution)/shard_map/pallas_call | solution.py:373
  21.9 0.0 collective-permute-done.4.refs_2_
  21.9 0.0 collective-permute-done.5.refs_3_
  22.0 8.0 %shard_map.81 = (f32[3552,256]{1,0:T(8,128)S(1)}, f32[3552,128]{1,0:T(8,128)S(1)}, f32[3552,256]{1,0:T(8,128)S(1)}, f32[3552,256]{1,0:T(8,128)S(1)}, f32[8,128]{1,0:T(8,128)S(1)}) custom-call(f32[3552,256]{1,0:T(8,128)S(1)} %get-tuple-element.33.refs_0_, f32[3552,128]{1,0:T(8,128)S(1)} %get-tuple-element.34.refs_1_, ...), custom_call_target="tpu_custom_call", output_to_operand_aliasing={{0}: (0, {}), {1}: (1, {})} | custom-call | tf_op jit(solution)/shard_map/pallas_call | solution.py:373
  30.0 2.0 %collective-permute-start.8 = (f32[8,128]{1,0:T(8,128)S(1)}, f32[8,128]{1,0:T(8,128)S(1)}, u32[]{:S(2)}, u32[]{:S(2)}) collective-permute-start(f32[8,128]{1,0:T(8,128)S(1)} %get-tuple-element.37), channel_id=1, source_target_pairs={{0,24},{8,16},{16,8},{24,0},{1,25},{9,17},{17,9},{25,1},{2,26},{10... | collective-permute-start | bytes 12296 | tf_op jit(solution)/shard_map/ppermute | solution.py:367
  31.9 1.4 %collective-permute-start.7 = (f32[8,128]{1,0:T(8,128)S(1)}, f32[8,128]{1,0:T(8,128)S(1)}, u32[]{:S(2)}, u32[]{:S(2)}) collective-permute-start(f32[8,128]{1,0:T(8,128)S(1)} %get-tuple-element.37), channel_id=1, source_target_pairs={{0,8},{8,0},{16,24},{24,16},{1,9},{9,1},{17,25},{25,17},{2,10},{10... | collective-permute-start | bytes 12296 | tf_op jit(solution)/shard_map/ppermute | solution.py:367
  33.4 0.1 collective-permute-start.6
  33.5 1.0 %collective-permute-done.8 = f32[8,128]{1,0:T(8,128)S(1)} collective-permute-done((f32[8,128]{1,0:T(8,128)S(1)}, f32[8,128]{1,0:T(8,128)S(1)}, u32[]{:S(2)}, u32[]{:S(2)}) %collective-permute-start.8) | collective-permute-done | bytes 4128 | tf_op jit(solution)/shard_map/ppermute | solution.py:367
  34.5 1.1 %collective-permute-done.7 = f32[8,128]{1,0:T(8,128)S(1)} collective-permute-done((f32[8,128]{1,0:T(8,128)S(1)}, f32[8,128]{1,0:T(8,128)S(1)}, u32[]{:S(2)}, u32[]{:S(2)}) %collective-permute-start.7) | collective-permute-done | bytes 4128 | tf_op jit(solution)/shard_map/ppermute | solution.py:367
  35.5 1.4 %collective-permute-done.6 = f32[8,128]{1,0:T(8,128)S(1)} collective-permute-done((f32[8,128]{1,0:T(8,128)S(1)}, f32[8,128]{1,0:T(8,128)S(1)}, u32[]{:S(2)}, u32[]{:S(2)}) %collective-permute-start.6) | collective-permute-done | bytes 4128 | tf_op jit(solution)/shard_map/ppermute | solution.py:367
  37.0 0.0 collective-permute-start.9
  37.0 1.2 %collective-permute-done.9 = f32[8,128]{1,0:T(8,128)S(1)} collective-permute-done((f32[8,128]{1,0:T(8,128)S(1)}, f32[8,128]{1,0:T(8,128)S(1)}, u32[]{:S(2)}, u32[]{:S(2)}) %collective-permute-start.9) | collective-permute-done | bytes 4128 | tf_op jit(solution)/shard_map/ppermute | solution.py:367
  38.1 3.9 %collective-permute-start.12 = (f32[8,128]{1,0:T(8,128)S(1)}, f32[8,128]{1,0:T(8,128)S(1)}, u32[]{:S(2)}, u32[]{:S(2)}) collective-permute-start(f32[8,128]{1,0:T(8,128)S(1)} %add.24), channel_id=1, source_target_pairs={{0,6},{1,7},{2,4},{3,5},{4,2},{5,3},{6,0},{7,1},{8,14},{9,15},{10,... | collective-permute-start | bytes 12296 | tf_op jit(solution)/shard_map/ppermute | solution.py:367
  42.0 0.0 collective-permute-start.11
  42.0 0.6 %collective-permute-start.10 = (f32[8,128]{1,0:T(8,128)S(1)}, f32[8,128]{1,0:T(8,128)S(1)}, u32[]{:S(2)}, u32[]{:S(2)}) collective-permute-start(f32[8,128]{1,0:T(8,128)S(1)} %add.24), channel_id=1, source_target_pairs={{0,4},{1,5},{2,6},{3,7},{4,0},{5,1},{6,2},{7,3},{8,12},{9,13},{10,... | collective-permute-start | bytes 12296 | tf_op jit(solution)/shard_map/ppermute | solution.py:367
  42.6 1.2 %shard_map.85 = (f32[16,32,256]{2,1,0:T(8,128)S(1)}, f32[16,32,256]{2,1,0:T(8,128)S(1)}) custom-call(f32[3552,256]{1,0:T(8,128)S(1)} %get-tuple-element.40.refs_0_.refs_4_, s32[3840,128]{1,0:T(8,128)S(1)} %shard_map.80.refs_4_.refs_1_, f32[1,256,256]{2,1,0:T(8,128)S(1)} %copy-done, f32[2,1,32,256]{3,2,1,0:T(8,128)S(1)} %copy-done.1, ...), custom_call_target="tpu_custom_call" | custom-call | tf_op jit(solution)/shard_map/pallas_call | solution.py:373
  43.8 1.2 %shard_map.84 = (f32[16,32,256]{2,1,0:T(8,128)S(1)}, f32[16,32,256]{2,1,0:T(8,128)S(1)}) custom-call(f32[3552,256]{1,0:T(8,128)S(1)} %get-tuple-element.40.refs_0_.refs_4_, s32[3840,128]{1,0:T(8,128)S(1)} %shard_map.80.refs_4_.refs_1_, f32[1,256,256]{2,1,0:T(8,128)S(1)} %copy-done, f32[2,1,32,256]{3,2,1,0:T(8,128)S(1)} %copy-done.1, ...), custom_call_target="tpu_custom_call" | custom-call | tf_op jit(solution)/shard_map/pallas_call | solution.py:373
  45.0 1.2 %shard_map.83 = (f32[16,32,256]{2,1,0:T(8,128)S(1)}, f32[16,32,256]{2,1,0:T(8,128)S(1)}) custom-call(f32[3552,256]{1,0:T(8,128)S(1)} %get-tuple-element.40.refs_0_.refs_4_, s32[3840,128]{1,0:T(8,128)S(1)} %shard_map.80.refs_4_.refs_1_, f32[1,256,256]{2,1,0:T(8,128)S(1)} %copy-done, f32[2,1,32,256]{3,2,1,0:T(8,128)S(1)} %copy-done.1, ...), custom_call_target="tpu_custom_call" | custom-call | tf_op jit(solution)/shard_map/pallas_call | solution.py:373
  46.1 1.2 %shard_map.82 = (f32[16,32,256]{2,1,0:T(8,128)S(1)}, f32[16,32,256]{2,1,0:T(8,128)S(1)}) custom-call(f32[3552,256]{1,0:T(8,128)S(1)} %get-tuple-element.40.refs_0_.refs_4_, s32[3840,128]{1,0:T(8,128)S(1)} %shard_map.80.refs_4_.refs_1_, f32[1,256,256]{2,1,0:T(8,128)S(1)} %copy-done, f32[2,1,32,256]{3,2,1,0:T(8,128)S(1)} %copy-done.1, ...), custom_call_target="tpu_custom_call" | custom-call | tf_op jit(solution)/shard_map/pallas_call | solution.py:373
  47.3 0.0 collective-permute-done.12
  47.3 0.0 collective-permute-done.11
  47.3 0.0 collective-permute-done.10
  47.4 2.9 %shard_map.86 = (f32[64,32,256]{2,1,0:T(8,128)}, f32[64,32,256]{2,1,0:T(8,128)}, f32[64,32,256]{2,1,0:T(8,128)}) custom-call(f32[8,128]{1,0:T(8,128)S(1)} %add_add_fusion.refs_0_, f32[64,32,256]{2,1,0:T(8,128)S(1)} %get-tuple-element.26.refs_0_.refs_5_.refs_1_, f32[3552,256]{1,0:T(8,128)S(1)} %get-tuple-element.38.refs_2_, ...), custom_call_target="tpu_custom_call" | custom-call | tf_op jit(solution)/shard_map/pallas_call | solution.py:373
  (4 shorter events, 0.0 us)
Async XLA Ops:
  0.6 15.5 %copy-start.3 = (s32[2,1,256,256]{3,2,1,0:T(8,128)S(1)}, s32[2,1,256,256]{3,2,1,0:T(8,128)}, u32[]{:S(2)}) copy-start(s32[2,1,256,256]{3,2,1,0:T(8,128)} %refs_0_.1) | copy-start | bytes 1572868
  2.3 16.2 %copy-start = (f32[1,256,256]{2,1,0:T(8,128)S(1)}, f32[1,256,256]{2,1,0:T(8,128)}, u32[]{:S(2)}) copy-start(f32[1,256,256]{2,1,0:T(8,128)} %refs_2_.9) | copy-start | bytes 786436
  2.3 16.2 %copy-start.1 = (f32[2,1,32,256]{3,2,1,0:T(8,128)S(1)}, f32[2,1,32,256]{3,2,1,0:T(8,128)}, u32[]{:S(2)}) copy-start(f32[2,1,32,256]{3,2,1,0:T(8,128)} %refs_3_.9) | copy-start | bytes 196612
  2.3 16.2 %copy-start.2 = (f32[2,1,32,256]{3,2,1,0:T(8,128)S(1)}, f32[2,1,32,256]{3,2,1,0:T(8,128)}, u32[]{:S(2)}) copy-start(f32[2,1,32,256]{3,2,1,0:T(8,128)} %refs_4_.7) | copy-start | bytes 196612
  2.4 10.2 %collective-permute-start.2 = (f32[5,64,256]{2,1,0:T(8,128)S(1)}, f32[5,64,256]{2,1,0:T(8,128)S(1)}, u32[]{:S(2)}, u32[]{:S(2)}) collective-permute-start(f32[5,64,256]{2,1,0:T(8,128)S(1)} %get-tuple-element.31), channel_id=1, source_target_pairs={{0,1},{1,2},{2,3},{3,4},{4,5},{5,6},{6,7},{7,0},{8,9},{9,10},{10,1... | collective-permute-start | bytes 983048 | tf_op jit(solution)/shard_map/ppermute | solution.py:353
  2.9 10.1 %collective-permute-start.3 = (f32[5,64,256]{2,1,0:T(8,128)S(1)}, f32[5,64,256]{2,1,0:T(8,128)S(1)}, u32[]{:S(2)}, u32[]{:S(2)}) collective-permute-start(f32[5,64,256]{2,1,0:T(8,128)S(1)} %get-tuple-element.32), channel_id=1, source_target_pairs={{0,7},{1,0},{2,1},{3,2},{4,3},{5,4},{6,5},{7,6},{8,15},{9,8},{10,9... | collective-permute-start | bytes 983048 | tf_op jit(solution)/shard_map/ppermute | solution.py:353
  7.0 13.1 %collective-permute-start = (f32[5,32,256]{2,1,0:T(8,128)S(1)}, f32[5,32,256]{2,1,0:T(8,128)S(1)}, u32[]{:S(2)}, u32[]{:S(2)}) collective-permute-start(f32[5,32,256]{2,1,0:T(8,128)S(1)} %get-tuple-element.29), channel_id=1, source_target_pairs={{0,8},{8,16},{16,24},{24,0},{1,9},{9,17},{17,25},{25,1},{2,10},{10... | collective-permute-start | bytes 491528 | tf_op jit(solution)/shard_map/ppermute | solution.py:353
  8.9 11.2 %collective-permute-start.1 = (f32[5,32,256]{2,1,0:T(8,128)S(1)}, f32[5,32,256]{2,1,0:T(8,128)S(1)}, u32[]{:S(2)}, u32[]{:S(2)}) collective-permute-start(f32[5,32,256]{2,1,0:T(8,128)S(1)} %get-tuple-element.30), channel_id=1, source_target_pairs={{0,24},{8,0},{16,8},{24,16},{1,25},{9,1},{17,9},{25,17},{2,26},{10... | collective-permute-start | bytes 491528 | tf_op jit(solution)/shard_map/ppermute | solution.py:353
  13.0 8.9 %collective-permute-start.4 = (f32[8,4,256]{2,1,0:T(4,128)S(1)}, f32[8,4,256]{2,1,0:T(4,128)S(1)}, u32[]{:S(2)}, u32[]{:S(2)}) collective-permute-start(f32[8,4,256]{2,1,0:T(4,128)S(1)} %get-tuple-element.35), channel_id=1, source_target_pairs={{0,8},{8,16},{16,24},{24,0},{1,9},{9,17},{17,25},{25,1},{2,10},{10... | collective-permute-start | bytes 98312 | tf_op jit(solution)/shard_map/ppermute | solution.py:353
  15.2 6.8 %collective-permute-start.5 = (f32[8,4,256]{2,1,0:T(4,128)S(1)}, f32[8,4,256]{2,1,0:T(4,128)S(1)}, u32[]{:S(2)}, u32[]{:S(2)}) collective-permute-start(f32[8,4,256]{2,1,0:T(4,128)S(1)} %get-tuple-element.36), channel_id=1, source_target_pairs={{0,24},{8,0},{16,8},{24,16},{1,25},{9,1},{17,9},{25,17},{2,26},{10... | collective-permute-start | bytes 98312 | tf_op jit(solution)/shard_map/ppermute | solution.py:353
  30.0 4.5 %collective-permute-start.8 = (f32[8,128]{1,0:T(8,128)S(1)}, f32[8,128]{1,0:T(8,128)S(1)}, u32[]{:S(2)}, u32[]{:S(2)}) collective-permute-start(f32[8,128]{1,0:T(8,128)S(1)} %get-tuple-element.37), channel_id=1, source_target_pairs={{0,24},{8,16},{16,8},{24,0},{1,25},{9,17},{17,9},{25,1},{2,26},{10... | collective-permute-start | bytes 12296 | tf_op jit(solution)/shard_map/ppermute | solution.py:367
  31.9 3.6 %collective-permute-start.7 = (f32[8,128]{1,0:T(8,128)S(1)}, f32[8,128]{1,0:T(8,128)S(1)}, u32[]{:S(2)}, u32[]{:S(2)}) collective-permute-start(f32[8,128]{1,0:T(8,128)S(1)} %get-tuple-element.37), channel_id=1, source_target_pairs={{0,8},{8,0},{16,24},{24,16},{1,9},{9,1},{17,25},{25,17},{2,10},{10... | collective-permute-start | bytes 12296 | tf_op jit(solution)/shard_map/ppermute | solution.py:367
  33.4 3.6 %collective-permute-start.6 = (f32[8,128]{1,0:T(8,128)S(1)}, f32[8,128]{1,0:T(8,128)S(1)}, u32[]{:S(2)}, u32[]{:S(2)}) collective-permute-start(f32[8,128]{1,0:T(8,128)S(1)} %get-tuple-element.37), channel_id=1, source_target_pairs={{0,16},{8,24},{16,0},{24,8},{1,17},{9,25},{17,1},{25,9},{2,18},{10... | collective-permute-start | bytes 12296 | tf_op jit(solution)/shard_map/ppermute | solution.py:367
  37.0 1.2 %collective-permute-start.9 = (f32[8,128]{1,0:T(8,128)S(1)}, f32[8,128]{1,0:T(8,128)S(1)}, u32[]{:S(2)}, u32[]{:S(2)}) collective-permute-start(f32[8,128]{1,0:T(8,128)S(1)} %add_add_fusion.1), channel_id=1, source_target_pairs={{0,1},{1,0},{2,3},{3,2},{4,5},{5,4},{6,7},{7,6},{8,9},{9,8},{10,11... | collective-permute-start | bytes 12296 | tf_op jit(solution)/shard_map/ppermute | solution.py:367
  38.1 9.2 %collective-permute-start.12 = (f32[8,128]{1,0:T(8,128)S(1)}, f32[8,128]{1,0:T(8,128)S(1)}, u32[]{:S(2)}, u32[]{:S(2)}) collective-permute-start(f32[8,128]{1,0:T(8,128)S(1)} %add.24), channel_id=1, source_target_pairs={{0,6},{1,7},{2,4},{3,5},{4,2},{5,3},{6,0},{7,1},{8,14},{9,15},{10,... | collective-permute-start | bytes 12296 | tf_op jit(solution)/shard_map/ppermute | solution.py:367
  42.0 5.3 %collective-permute-start.11 = (f32[8,128]{1,0:T(8,128)S(1)}, f32[8,128]{1,0:T(8,128)S(1)}, u32[]{:S(2)}, u32[]{:S(2)}) collective-permute-start(f32[8,128]{1,0:T(8,128)S(1)} %add.24), channel_id=1, source_target_pairs={{0,2},{1,3},{2,0},{3,1},{4,6},{5,7},{6,4},{7,5},{8,10},{9,11},{10,... | collective-permute-start | bytes 12296 | tf_op jit(solution)/shard_map/ppermute | solution.py:367
  42.0 5.3 %collective-permute-start.10 = (f32[8,128]{1,0:T(8,128)S(1)}, f32[8,128]{1,0:T(8,128)S(1)}, u32[]{:S(2)}, u32[]{:S(2)}) collective-permute-start(f32[8,128]{1,0:T(8,128)S(1)} %add.24), channel_id=1, source_target_pairs={{0,4},{1,5},{2,6},{3,7},{4,0},{5,1},{6,2},{7,3},{8,12},{9,13},{10,... | collective-permute-start | bytes 12296 | tf_op jit(solution)/shard_map/ppermute | solution.py:367
